TPU v7x, 256 devices: a whole 4x4x8 slice. The times are simulated.
256 devices in a mesh: expert: 64 (over x_lo, z, y), tensor: 4 (over x_hi, core).
Axes of the slice: x: 4 (x_hi: 2, x_lo: 2; x = x_hi * 2 + x_lo), y: 4, z: 8, core: 2. Of those that a mesh axis runs over, the one named last changes fastest.
Arguments:
- tokens: bfloat16 [8192, 2048], P('expert', 'tensor'), may hold values from -6 to 6
- grad_out: bfloat16 [8192, 2048], P('expert', 'tensor'), may hold values from -6 to 6
- route_weights: float32 [8192, 8], P('expert'), may hold values from 0.02 to 0.5
- expert_ids: int32 [8192, 8], P('expert'), may hold values from 0 to 127, all different within a row; in each aligned block of 128 rows (0 to 127, 128 to 255, ...) at most 12 rows name the same one
- gate_weight: bfloat16 [128, 2048, 768], P('expert', None, 'tensor'), may hold values from -0.125 to 0.125
- up_weight: bfloat16 [128, 2048, 768], P('expert', None, 'tensor'), may hold values from -0.125 to 0.125
- down_weight: bfloat16 [128, 768, 2048], P('expert', 'tensor'), may hold values from -0.21875 to 0.21875
- gate_adapter_first: bfloat16 [128, 2048, 64], P('expert'), may hold values from -0.125 to 0.125
- gate_adapter_second: bfloat16 [128, 64, 768], P('expert', None, 'tensor'), may hold values from -0.75 to 0.75
- up_adapter_first: bfloat16 [128, 2048, 64], P('expert'), may hold values from -0.125 to 0.125
- up_adapter_second: bfloat16 [128, 64, 768], P('expert', None, 'tensor'), may hold values from -0.75 to 0.75
- down_adapter_first: bfloat16 [128, 768, 64], P('expert', 'tensor'), may hold values from -0.21875 to 0.21875
- down_adapter_second: bfloat16 [128, 64, 2048], P('expert'), may hold values from -0.75 to 0.75
Outputs:
- grad_tokens: bfloat16 [8192, 2048], P('expert', 'tensor')
- gate_first_gradient: float32 [128, 2048, 64], P('expert', 'tensor')
- gate_second_gradient: float32 [128, 64, 768], P('expert', None, 'tensor')
- up_first_gradient: float32 [128, 2048, 64], P('expert', 'tensor')
- up_second_gradient: float32 [128, 64, 768], P('expert', None, 'tensor')
- down_first_gradient: float32 [128, 768, 64], P('expert', 'tensor')
- down_second_gradient: float32 [128, 64, 2048], P('expert', None, 'tensor')
Inputs may be any that keep to these rules, and one draw needn't show every extreme that they name: `expert_ids`: each token names 8 different experts. Among the 128 rows of one device no expert is named more than 12 times, a bound that some block reaches.
All inputs are finite; a program needn't handle non-finite values.
Results may differ from a plain program's by a relative error of at most 0.012.
Values may be sent and summed in bfloat16 or wider, within the bound.
No kernel may reach another device: no remote copies, remote signals or barrier semaphores. Data moves between devices by JAX's collectives and lax.ppermute only.
A program may use at most 128 MiB of HBM per device.

v0:
```python
import jax
import jax.numpy as jnp
from jax import lax
from jax.experimental import pallas as pl
from jax.experimental.pallas import tpu as pltpu
from jax.sharding import PartitionSpec as P


bf16 = jnp.bfloat16
f32 = jnp.float32
SCALE = 0.5
NZ, NY, CAP, TOP = 8, 4, 12, 8
AXES = ("expert", "tensor")
HALF = CAP * NZ // 2


def pairs(fn):
    out = []
    for xl in range(2):
        for z in range(NZ):
            for y in range(NY):
                for xh in range(2):
                    for c in range(2):
                        a, b, d, e, f = fn(xl, z, y, xh, c)
                        src = ((xl * NZ + z) * NY + y) * 4 + xh * 2 + c
                        dst = ((a * NZ + b) * NY + d) * 4 + e * 2 + f
                        out.append((src, dst))
    return out


def inverse(perm):
    return [(d, s) for s, d in perm]


Z_BY = [pairs(lambda xl, z, y, xh, c, s=s: (xl, (z + s) % NZ, y, xh, c)) for s in range(NZ)]
Y_BY = [pairs(lambda xl, z, y, xh, c, s=s: (xl, z, (y + s) % NY, xh, c)) for s in range(NY)]
X_BY = [
    pairs(lambda xl, z, y, xh, c, i=i, j=j: (xl ^ j, z, y, xh ^ i, c))
    for i in range(2)
    for j in range(2)
]
X_HALF = pairs(lambda xl, z, y, xh, c: (xl, z, y, 1 - xh, c))
CORE = pairs(lambda xl, z, y, xh, c: (xl, z, y, xh, 1 - c))


def move(x, perm):
    return lax.ppermute(x, AXES, perm)


def dot(a, b, ca, cb):
    return lax.dot_general(a, b, (((ca,), (cb,)), ((), ())), preferred_element_type=f32)


def pick(array, index):
    return lax.dynamic_index_in_dim(array, index, 0, keepdims=False)


VMEM = pl.BlockSpec(memory_space=pltpu.VMEM)


def grant(mib):
    return pltpu.CompilerParams(vmem_limit_bytes=mib << 20)


def blocks_of(refs):
    n = refs[0].shape[0]
    starts = ((0, 0), (1, 0), (2, 0), (3, 0), (4, 0), (4, n), (5, 0), (5, n))
    return [(refs[k], start) for k, start in starts]


def select_kernel(scalars, *refs):
    packed, (*outs, target_ref, slot_weight_ref) = blocks_of(refs[:6]), refs[6:]
    select_refs, weight_refs, out_refs = outs[:2], outs[2:4], outs[4:]
    rows = (refs[0].shape[0] - TOP) // 2
    q = lax.broadcasted_iota(jnp.int32, (16, rows), 0)
    q_y = jnp.bitwise_and(scalars[6] + jnp.right_shift(q, 2), NY - 1)
    q_xh = jnp.bitwise_xor(scalars[0], jnp.bitwise_and(jnp.right_shift(q, 1), 1))
    q_xl = jnp.bitwise_xor(scalars[8], jnp.bitwise_and(q, 1))
    number = (2 * ((q_xl * NZ + scalars[7]) * NY + q_y) + q_xh).astype(f32)
    earlier = (
        lax.broadcasted_iota(jnp.int32, (rows, rows), 0)
        < lax.broadcasted_iota(jnp.int32, (rows, rows), 1)
    ).astype(f32).astype(bf16)
    for b in range(NZ):
        ref, start = packed[b]
        meta = ref[start + 2 * rows : start + 2 * rows + TOP, :].astype(f32)
        ids = meta[:, :rows]
        weight = meta[:, rows : 2 * rows] + meta[:, 2 * rows : 3 * rows] + meta[:, 3 * rows :]
        picked = jnp.zeros(number.shape, f32)
        slot_weight = jnp.zeros(number.shape, f32)
        for k in range(TOP):
            match = ids[k : k + 1, :] == number
            picked = jnp.where(match, 1.0, picked)
            slot_weight = jnp.where(match, weight[k : k + 1, :], slot_weight)
        before = dot(picked.astype(bf16), earlier, 1, 0)
        target = jnp.where(picked > 0.0, before + float(CAP * (b % 4)), -1.0)
        for q in range(16):
            target_ref[q, :, b * rows : (b + 1) * rows] = target[q : q + 1, :]
            slot_weight_ref[q, :, b * rows : (b + 1) * rows] = slot_weight[q : q + 1, :]
    place = lax.broadcasted_iota(jnp.int32, (HALF, rows), 0).astype(f32)

    def expert(q, _):
        start = pl.multiple_of(q * HALF, HALF)
        for h in range(2):
            total = jnp.zeros((HALF, rows), f32)
            for b in range(4):
                lanes = slice((4 * h + b) * rows, (4 * h + b + 1) * rows)
                hit = target_ref[q, :, lanes] == place
                select_refs[h][pl.ds(start, HALF), b * rows : (b + 1) * rows] = jnp.where(
                    hit, 1.0, 0.0
                ).astype(bf16)
                total = total + jnp.where(hit, slot_weight_ref[q, :, lanes], 0.0)
            weight_refs[h][pl.ds(start, HALF), :] = jnp.broadcast_to(
                jnp.sum(total, axis=1, keepdims=True), (HALF, rows)
            )
        return 0

    lax.fori_loop(0, 16, expert, 0)
    for h in range(2):
        every = jnp.concatenate(
            [p[start : start + rows, :] for p, start in packed[4 * h : 4 * h + 4]], axis=0
        )
        for s in range(NY):
            part = dot(select_refs[h][s * 4 * HALF : (s + 1) * 4 * HALF, :], every, 1, 0)
            out_refs[s][h * 4 * HALF : (h + 1) * 4 * HALF, :] = part.astype(bf16)


def select_in(scalars, packed, rows, width):
    slots = 16 * HALF
    shapes = [((slots, 4 * rows), bf16)] * 2 + [((slots, rows), f32)] * 2
    shapes += [((8 * HALF, width), bf16)] * NY
    return pl.pallas_call(
        select_kernel,
        in_specs=[SCALARS] + [VMEM] * 6,
        out_specs=[VMEM] * len(shapes),
        out_shape=[jax.ShapeDtypeStruct(shape, dtype) for shape, dtype in shapes],
        scratch_shapes=[pltpu.VMEM((16, 1, NZ * rows), f32), pltpu.VMEM((16, 1, NZ * rows), f32)],
        compiler_params=grant(16),
        name="select_in",
    )(scalars, *packed)


def select_grad_kernel(*refs):
    select_refs, weight_refs, out_refs = refs[:2], refs[2:4], refs[10:]
    packed = blocks_of(refs[4:10])
    rows = (refs[4].shape[0] - TOP) // 2
    for h in range(2):
        every = jnp.concatenate(
            [p[start + rows : start + 2 * rows, :] for p, start in packed[4 * h : 4 * h + 4]],
            axis=0,
        )
        for s in range(NY):
            part = slice(s * 4 * HALF, (s + 1) * 4 * HALF)
            product = dot(select_refs[h][part, :], every, 1, 0) * weight_refs[h][part, :1]
            out_refs[s][h * 4 * HALF : (h + 1) * 4 * HALF, :] = product.astype(bf16)


def select_grad(selects, weights, packed, width):
    return pl.pallas_call(
        select_grad_kernel,
        in_specs=[VMEM] * 10,
        out_specs=[VMEM] * NY,
        out_shape=[jax.ShapeDtypeStruct((8 * HALF, width), bf16) for _ in range(NY)],
        compiler_params=grant(16),
        name="select_grad",
    )(*selects, *weights, *packed)


def combine_kernel(*refs):
    select_refs, pieces, (down_ref, up_ref, far_ref, near_ref) = refs[:2], refs[2:6], refs[6:]
    half = near_ref.shape[0] // 3
    for h in (1, 0):
        values = jnp.concatenate(
            [p[h * 4 * HALF : (h + 1) * 4 * HALF, :] for p in pieces], axis=0
        )
        total = dot(select_refs[h][...], values, 0, 0)
        if h == 1:
            down_ref[...] = total[: 2 * half, :].astype(bf16)
            up_ref[...] = total[2 * half :, :].astype(bf16)
        else:
            near_ref[...] = total[: 3 * half, :]
            far_ref[...] = total[3 * half :, :].astype(bf16)


def combine(selects, pieces, rows, width):
    shapes = [((2 * rows, width), bf16)] * 2 + [((rows, width), bf16), ((3 * rows, width), f32)]
    return pl.pallas_call(
        combine_kernel,
        in_specs=[VMEM] * 6,
        out_specs=[VMEM] * 4,
        out_shape=[jax.ShapeDtypeStruct(shape, dtype) for shape, dtype in shapes],
        compiler_params=grant(16),
        name="combine",
    )(*selects, *pieces)


SCALARS = pl.BlockSpec(memory_space=pltpu.SMEM)


def to_chips_kernel(*refs):
    for s in range(NY):
        for h in range(2):
            for k in range(4):
                refs[4 + k][(2 * s + h) * HALF : (2 * s + h + 1) * HALF, :] = refs[s][
                    (4 * h + k) * HALF : (4 * h + k + 1) * HALF, :
                ]


def from_chips_kernel(*refs):
    for s in range(NY):
        for h in range(2):
            for k in range(4):
                refs[4 + s][(4 * h + k) * HALF : (4 * h + k + 1) * HALF, :] = refs[k][
                    (2 * s + h) * HALF : (2 * s + h + 1) * HALF, :
                ]


def regroup(kernel, pieces):
    return pl.pallas_call(
        kernel,
        in_specs=[VMEM] * 4,
        out_specs=[VMEM] * 4,
        out_shape=[jax.ShapeDtypeStruct(p.shape, p.dtype) for p in pieces],
        compiler_params=grant(8),
    )(*pieces)


def split_kernel(scalars, *refs):
    sent, (cross_ref, kept_ref) = refs[:4], refs[4:]
    for swapped in range(2):

        @pl.when(scalars[5] == swapped)
        def _(swapped=swapped):
            for i in range(2):
                kept_ref[i] = sent[2 * i + swapped][...]
                cross_ref[i] = sent[2 * i + 1 - swapped][...]


def split(scalars, sent):
    shape = jax.ShapeDtypeStruct((2, *sent[0].shape), bf16)
    return pl.pallas_call(
        split_kernel,
        in_specs=[SCALARS] + [VMEM] * 4,
        out_specs=[VMEM] * 2,
        out_shape=[shape] * 2,
        compiler_params=grant(8),
        name="split_cores",
    )(scalars, *sent)


def join_kernel(scalars, own_ref, crossed_ref, *home):
    for swapped in range(2):

        @pl.when(scalars[5] == swapped)
        def _(swapped=swapped):
            for i in range(2):
                home[2 * i + swapped][...] = own_ref[i]
                home[2 * i + 1 - swapped][...] = crossed_ref[i]


def join(scalars, own, crossed):
    return pl.pallas_call(
        join_kernel,
        in_specs=[SCALARS, VMEM, VMEM],
        out_specs=[VMEM] * 4,
        out_shape=[jax.ShapeDtypeStruct(own.shape[1:], bf16)] * 4,
        compiler_params=grant(8),
        name="join_cores",
    )(scalars, own, crossed)


def whole(shape):
    return pl.BlockSpec(shape, lambda g, s: (0,) * len(shape))


def stack(refs):
    return jnp.concatenate([r[0] if len(r.shape) == 3 else r[...] for r in refs], axis=0)


def part_of(parts, step):
    return jnp.where(step % 2 == 0, parts[0][0], parts[1][0])


def part_specs(rows, width, block):
    return [pl.BlockSpec((1, rows, width), lambda g, s: (block(g) // 2, 0, 0))] * 2


def forward_kernel(scalars, *refs):
    parts, (gates, ups, firsts), seconds = refs[:2], (refs[2:6], refs[6:10], refs[10:12]), refs[12]
    gate_ref, up_ref, hidden_ref, lora_gate_ref, lora_up_ref, down_lora_ref, acc = refs[13:]
    step = pl.program_id(0)
    rank = seconds.shape[0] // 3
    units = seconds.shape[1]
    product = dot(part_of(parts, step), stack((*gates, *ups, *firsts)), 1, 1)
    acc[...] = jnp.where(step == 0, 0.0, acc[...]) + product

    @pl.when(step == 3)
    def _():
        lora_gate = acc[:, 2 * units : 2 * units + rank].astype(bf16)
        lora_up = acc[:, 2 * units + rank :].astype(bf16)
        gate = acc[:, :units] + SCALE * dot(lora_gate, seconds[:rank, :], 1, 0)
        up = acc[:, units : 2 * units] + SCALE * dot(lora_up, seconds[rank : 2 * rank, :], 1, 0)
        hidden = (gate * jax.nn.sigmoid(gate) * up).astype(bf16)
        gate_ref[...] = gate
        up_ref[...] = up
        hidden_ref[...] = hidden
        lora_gate_ref[...] = lora_gate
        lora_up_ref[...] = lora_up
        down_lora_ref[...] = dot(hidden, seconds[2 * rank :, :], 1, 1).astype(bf16)


def weight_specs(count, units, width, block, which=0):
    own = pl.BlockSpec((1, units, width), lambda g, s: (s[0], 0, s[1 + block(g)]))
    moved = pl.BlockSpec((units, width), lambda g, s: (which, s[1 + block(g)]))
    return [own] + [moved] * (count - 1)


def expert_forward(scalars, parts, gates, ups, firsts, seconds):
    rows, width = parts[0].shape[1:]
    rank, units = seconds.shape[0] // 3, seconds.shape[1]
    piece = units // 4
    block = lambda g: g
    specs = part_specs(rows, width, block)
    specs += weight_specs(4, piece, width, block, 0) + weight_specs(4, piece, width, block, 1)
    specs += weight_specs(1, rank, width, block) * 2
    specs += [whole(seconds.shape)]
    shapes = [((rows, units), f32)] * 2 + [((rows, units), bf16)] + [((rows, rank), bf16)] * 3
    return pl.pallas_call(
        forward_kernel,
        grid_spec=pltpu.PrefetchScalarGridSpec(
            num_scalar_prefetch=1,
            grid=(4,),
            in_specs=specs,
            out_specs=[whole(shape) for shape, _ in shapes],
            scratch_shapes=[pltpu.VMEM((rows, 2 * units + 2 * rank), f32)],
        ),
        out_shape=[jax.ShapeDtypeStruct(shape, dtype) for shape, dtype in shapes],
        compiler_params=grant(28),
        name="expert_forward",
    )(scalars, *parts, *gates, *ups, *firsts, seconds)


def backward_kernel(scalars, *refs):
    cots, parts, late_cots, downs, refs = refs[:2], refs[2:4], refs[4:6], refs[6:11], refs[11:]
    gates, ups, firsts, seconds, refs = refs[:4], refs[4:8], refs[8:10], refs[10], refs[11:]
    gate_ref, up_ref, hidden_ref, lora_gate_ref, lora_up_ref, down_lora_ref, *refs = refs
    own_ref, cross_ref, feature_ref, by_hidden_ref, acc, left = refs
    step = pl.program_id(0)
    rank = seconds.shape[0] // 3
    units = seconds.shape[1]

    @pl.when(step < 4)
    def _():
        product = dot(part_of(cots, step), stack(downs), 1, 1)
        acc[...] = jnp.where(step == 0, 0.0, acc[...]) + product

    @pl.when(step == 3)
    def _():
        gate, up = gate_ref[...], up_ref[...]
        back_lora = acc[:, units:].astype(bf16)
        grad_hidden = acc[:, :units] + SCALE * dot(back_lora, seconds[2 * rank :, :], 1, 0)
        sigma = jax.nn.sigmoid(gate)
        grad_gate = (grad_hidden * up * sigma * (1.0 + gate * (1.0 - sigma))).astype(bf16)
        grad_up = (grad_hidden * (gate * sigma)).astype(bf16)
        left[:, :units] = grad_gate
        left[:, units : 2 * units] = grad_up
        gate_back = dot(grad_gate, seconds[:rank, :], 1, 1)
        up_back = dot(grad_up, seconds[rank : 2 * rank, :], 1, 1)
        left[:, 2 * units :] = (
            jnp.concatenate((gate_back, up_back), axis=1).astype(bf16).astype(f32) * SCALE
        ).astype(bf16)
        by_hidden_ref[:rank, :] = SCALE * dot(lora_gate_ref[...], grad_gate, 0, 0)
        by_hidden_ref[rank : 2 * rank, :] = SCALE * dot(lora_up_ref[...], grad_up, 0, 0)
        by_hidden_ref[2 * rank :, :] = SCALE * dot(back_lora, hidden_ref[...], 0, 0)

    @pl.when(step >= 4)
    def _():
        weights = stack((*gates, *ups, *firsts))
        result = dot(left[...], weights, 1, 0).astype(bf16)
        for k, ref in enumerate((own_ref, cross_ref)):

            @pl.when(step % 2 == k)
            def _(ref=ref):
                ref[0] = result

        feature_ref[: 2 * rank, :] = dot(left[:, 2 * units :], part_of(parts, step), 0, 0)
        feature_ref[2 * rank :, :] = SCALE * dot(down_lora_ref[...], part_of(late_cots, step), 0, 0)


def expert_backward(scalars, cots, parts, downs, down_second, gates, ups, firsts, seconds, saved):
    rows, width = parts[0].shape[1:]
    rank, units = seconds.shape[0] // 3, seconds.shape[1]
    piece = units // 4
    early = lambda g: jnp.minimum(g, 3)
    late = lambda g: jnp.maximum(g - 4, 0)
    specs = part_specs(rows, width, early) + part_specs(rows, width, late) * 2
    specs += weight_specs(4, piece, width, early, 2) + weight_specs(1, rank, width, early)
    specs += weight_specs(4, piece, width, late, 0) + weight_specs(4, piece, width, late, 1)
    specs += weight_specs(1, rank, width, late) * 2
    specs += [whole(seconds.shape)] + [whole(s.shape) for s in saved]
    return pl.pallas_call(
        backward_kernel,
        grid_spec=pltpu.PrefetchScalarGridSpec(
            num_scalar_prefetch=1,
            grid=(8,),
            in_specs=specs,
            out_specs=[
                pl.BlockSpec((1, rows, width), lambda g, s: (late(g) // 2, 0, 0)),
                pl.BlockSpec((1, rows, width), lambda g, s: (late(g) // 2, 0, 0)),
                pl.BlockSpec((3 * rank, width), lambda g, s: (0, late(g))),
                whole((3 * rank, units)),
            ],
            scratch_shapes=[
                pltpu.VMEM((rows, units + rank), f32),
                pltpu.VMEM((rows, 2 * units + 2 * rank), bf16),
            ],
        ),
        out_shape=[
            jax.ShapeDtypeStruct((2, rows, width), bf16),
            jax.ShapeDtypeStruct((2, rows, width), bf16),
            jax.ShapeDtypeStruct((3 * rank, 4 * width), f32),
            jax.ShapeDtypeStruct((3 * rank, units), f32),
        ],
        compiler_params=grant(36),
        name="expert_backward",
    )(scalars, *cots, *parts, *cots, *downs, down_second, *gates, *ups, *firsts, seconds, *saved)


def local(
    tokens,
    grad_out,
    route_weights,
    expert_ids,
    gate_weight,
    up_weight,
    down_weight,
    gate_adapter_first,
    gate_adapter_second,
    up_adapter_first,
    up_adapter_second,
    down_adapter_first,
    down_adapter_second,
):
    e_index = lax.axis_index("expert")
    t_index = lax.axis_index("tensor")
    xl = e_index // (NZ * NY)
    z = (e_index // NY) % NZ
    y = e_index % NY
    xh = t_index // 2
    c = t_index % 2
    rows, width = tokens.shape
    features = [2 * (xh ^ i) + (c ^ j) for i in range(2) for j in range(2)]
    scalars = jnp.stack([xh, *features, xl ^ c, y, z, xl]).astype(jnp.int32)

    gate_t = jnp.swapaxes(gate_weight, 1, 2)
    up_t = jnp.swapaxes(up_weight, 1, 2)
    first_t = jnp.swapaxes(down_adapter_first, 1, 2)

    def of_expert(e, weights):
        seconds = (gate_adapter_second, up_adapter_second, first_t)
        small = jnp.concatenate([pick(w, e) for w in seconds], axis=1)
        small = jnp.pad(small, ((0, 0), (0, weights[0].shape[2] - small.shape[1])))
        return jnp.concatenate([*(pick(w, e) for w in weights), small], axis=0)

    big_x = move(of_expert(1 - xh, (gate_t, up_t, down_weight)), X_HALF)

    ids_t = expert_ids.T.astype(bf16)
    w_t = route_weights.T
    w_hi = lax.reduce_precision(w_t, 8, 7)
    w_rest = w_t - w_hi
    w_mid = lax.reduce_precision(w_rest, 8, 7)
    w_low = w_rest - w_mid
    meta = jnp.concatenate(
        (ids_t, w_hi.astype(bf16), w_mid.astype(bf16), w_low.astype(bf16)), axis=1
    )
    packed = jnp.concatenate((tokens, grad_out, meta), axis=0)
    low, high = move(packed, Z_BY[2]), move(packed, Z_BY[6])
    far = move(packed, Z_BY[4])
    after = move(jnp.concatenate((packed, low), axis=0), Z_BY[1])
    ahead = move(jnp.concatenate((packed, high), axis=0), Z_BY[7])
    everything = (packed, low, high, far, after, ahead)

    def to_chip(routed):
        return [routed[0]] + [move(routed[s], Y_BY[s]) for s in range(1, NY)]

    def over_x(got):
        sent = regroup(to_chips_kernel, got)
        return [sent[0]] + [move(sent[k], X_BY[k]) for k in range(1, 4)]

    def to_core(sent):
        crossed, kept = split(scalars, sent)
        return kept, move(crossed, CORE)

    *chosen, in_0, in_1, in_2, in_3 = select_in(scalars, everything, rows, width)
    selects, row_weights = chosen[:2], chosen[2:]

    in_0, gate_own, up_own, down_own = lax.optimization_barrier((in_0, gate_t, up_t, down_weight))
    big_own = of_expert(xh, (gate_own, up_own, down_own))
    big_c = move(big_own, CORE)

    in_sent = over_x(to_chip((in_0, in_1, in_2, in_3)))
    grad_out_0, *grad_rest = select_grad(selects, row_weights, everything, width)
    grad_got = to_chip((grad_out_0, *grad_rest))
    big_xc = move(big_x, CORE)
    gates, ups, downs = ((w, big_x, big_c, big_xc) for w in (gate_t, up_t, down_weight))
    units = gate_weight.shape[2]
    seconds = [
        jnp.concatenate(
            [w[3 * units :, k * units : (k + 1) * units] for w in (big_own, big_x, big_c, big_xc)],
            axis=1,
        )
        for k in range(3)
    ]
    seconds = jnp.concatenate(seconds, axis=0)
    firsts = (jnp.swapaxes(gate_adapter_first, 1, 2), jnp.swapaxes(up_adapter_first, 1, 2))

    in_parts = to_core(in_sent)
    grad_sent = over_x(grad_got)

    saved = expert_forward(scalars, in_parts, gates, ups, firsts, seconds)
    tied = lax.optimization_barrier((*grad_sent, *saved))
    grad_sent, saved = tied[:4], tied[4:]
    grad_parts = to_core(grad_sent)
    own_grad, cross_grad, by_feature, by_hidden = expert_backward(
        scalars, grad_parts, in_parts, downs, down_adapter_second, gates, ups, firsts, seconds, saved
    )

    home = join(scalars, own_grad, move(cross_grad, CORE))
    home = [home[0]] + [move(home[k], X_BY[k]) for k in range(1, 4)]

    by_feature, by_hidden, *home = lax.optimization_barrier((by_feature, by_hidden, *home))

    feature = [by_feature[:, k * width : (k + 1) * width] for k in range(4)]
    mine = jnp.concatenate((feature[0], feature[2], by_hidden[:, : 2 * units]), axis=1)
    other = jnp.concatenate((feature[1], feature[3], by_hidden[:, 2 * units :]), axis=1)
    total = mine + move(other, CORE)
    keep = jnp.concatenate(
        (total[:, :width], total[:, 2 * width : 2 * width + units]), axis=1
    )
    give = jnp.concatenate((total[:, width : 2 * width], total[:, 2 * width + units :]), axis=1)
    came = move(give, X_HALF)
    first = jnp.where(xh == 0, keep, came)
    second = jnp.where(xh == 0, came, keep)
    both = jnp.stack((first, second), axis=0)
    f_part, h_part = both[:, :, :width], both[:, :, width:]

    came_y = regroup(from_chips_kernel, home)
    came_y = [came_y[0]] + [move(came_y[s], inverse(Y_BY[s])) for s in range(1, NY)]
    down_pair, up_pair, far, near = combine(selects, came_y, rows, width)
    far = move(far, Z_BY[4])
    from_up = move(down_pair, Z_BY[7]).astype(f32)
    from_down = move(up_pair, Z_BY[1]).astype(f32)
    to_low = (near[rows : 2 * rows] + from_up[rows:]).astype(bf16)
    to_high = (near[2 * rows :] + from_down[rows:]).astype(bf16)
    result = near[:rows] + from_up[:rows] + from_down[:rows] + far.astype(f32)
    result = result + move(to_low, Z_BY[6]).astype(f32) + move(to_high, Z_BY[2]).astype(f32)
    return (
        result.astype(bf16),
        jnp.swapaxes(f_part[:, :64], 1, 2),
        h_part[:, :64],
        jnp.swapaxes(f_part[:, 64:128], 1, 2),
        h_part[:, 64:128],
        jnp.swapaxes(h_part[:, 128:], 1, 2),
        f_part[:, 128:],
    )


def solution(mesh):
    return jax.shard_map(
        local,
        mesh=mesh,
        in_specs=(
            P("expert", "tensor"),
            P("expert", "tensor"),
            P("expert", None),
            P("expert", None),
            P("expert", None, "tensor"),
            P("expert", None, "tensor"),
            P("expert", "tensor", None),
            P("expert", None, None),
            P("expert", None, "tensor"),
            P("expert", None, None),
            P("expert", None, "tensor"),
            P("expert", "tensor", None),
            P("expert", None, None),
        ),
        out_specs=(
            P("expert", "tensor"),
            P("expert", "tensor", None),
            P("expert", None, "tensor"),
            P("expert", "tensor", None),
            P("expert", None, "tensor"),
            P("expert", "tensor", None),
            P("expert", None, "tensor"),
        ),
        check_vma=False,
    )
```

profile of v0, /device:TPU:24, one launch (start us, length us, event | category | flops | bytes accessed | tf_op | source)
XLA Modules:
  0.0 243.4 jit_solution(14145883454095538049)
XLA Ops:
  0.7 1.3 dynamic-slice_bitcast_fusion.3
  3.8 1.6 pad_maximum_fusion
  5.4 3.0 %collective-permute-start.18 = (bf16[640,2048]{1,0:T(8,128)(2,1)}, bf16[640,2048]{1,0:T(8,128)(2,1)S(1)}, u32[]{:S(2)}, u32[]{:S(2)}) collective-permute-start(bf16[640,2048]{1,0:T(8,128)(2,1)} %pad_maximum_fusion), channel_id=1, source_target_pairs={{0,2},{1,3},{2,0},{3,1},{4,6},{5,7},{6,4},{7,5},{8,10},{9,11},{10,... | collective-permute-start | bytes 7864328 | tf_op jit(solution)/shard_map/ppermute | solution.py:47
  8.5 6.4 %collective-permute-start.1 = (bf16[264,512]{1,0:T(8,128)(2,1)S(1)}, bf16[264,512]{1,0:T(8,128)(2,1)S(1)}, u32[]{:S(2)}, u32[]{:S(2)}) collective-permute-start(bf16[264,512]{1,0:T(8,128)(2,1)S(1)} %maximum_maximum_fusion.2.refs_0_.refs_4_), channel_id=1, source_target_pairs={{0,96},{1,97},{2,98},{3,99},{4,100},{5,101},{6,102},{7,103},{8,104... | collective-permute-start | bytes 811016 | tf_op jit(solution)/shard_map/ppermute | solution.py:47
  14.8 11.3 %collective-permute-done.1.refs_2_.refs_6_ = bf16[264,512]{1,0:T(8,128)(2,1)S(1)} collective-permute-done((bf16[264,512]{1,0:T(8,128)(2,1)S(1)}, bf16[264,512]{1,0:T(8,128)(2,1)S(1)}, u32[]{:S(2)}, u32[]{:S(2)}) %collective-permute-start.1) | collective-permute-done | bytes 270368 | tf_op jit(solution)/shard_map/ppermute | solution.py:47
  26.1 3.8 %collective-permute-done.refs_1_.refs_5_ = bf16[264,512]{1,0:T(8,128)(2,1)S(1)} collective-permute-done((bf16[264,512]{1,0:T(8,128)(2,1)S(1)}, bf16[264,512]{1,0:T(8,128)(2,1)S(1)}, u32[]{:S(2)}, u32[]{:S(2)}) %collective-permute-start) | collective-permute-done | bytes 270368 | tf_op jit(solution)/shard_map/ppermute | solution.py:47
  31.4 1.7 collective-permute-start.3
  34.1 20.5 %collective-permute-done.2.refs_3_.refs_7_ = bf16[264,512]{1,0:T(8,128)(2,1)} collective-permute-done((bf16[264,512]{1,0:T(8,128)(2,1)S(1)}, bf16[264,512]{1,0:T(8,128)(2,1)}, u32[]{:S(2)}, u32[]{:S(2)}) %collective-permute-start.2) | collective-permute-done | bytes 270368 | tf_op jit(solution)/shard_map/ppermute | solution.py:47
  54.6 3.1 %collective-permute-done.3.refs_4_.refs_8_ = bf16[528,512]{1,0:T(8,128)(2,1)} collective-permute-done((bf16[528,512]{1,0:T(8,128)(2,1)}, bf16[528,512]{1,0:T(8,128)(2,1)}, u32[]{:S(2)}, u32[]{:S(2)}) %collective-permute-start.3) | collective-permute-done | bytes 540704 | tf_op jit(solution)/shard_map/ppermute | solution.py:47
  57.7 4.2 %select_in.1 = (bf16[768,512]{1,0:T(8,128)(2,1)S(1)}, bf16[768,512]{1,0:T(8,128)(2,1)S(1)}, f32[768,128]{1,0:T(8,128)S(1)}, f32[768,128]{1,0:T(8,128)S(1)}, bf16...) custom-call(s32[9]{0:T(128)S(1)} %stack.48.scalars, ...), custom_call_target="tpu_custom_call" | custom-call | tf_op jit(solution)/shard_map/select_in/pallas_call | solution.py:132
  62.0 1.3 copy-done.5
  63.3 1.3 dynamic-slice_bitcast_fusion
  65.8 2.7 %collective-permute-start.12 = (bf16[384,512]{1,0:T(8,128)(2,1)S(1)}, bf16[384,512]{1,0:T(8,128)(2,1)S(1)}, u32[]{:S(2)}, u32[]{:S(2)}) collective-permute-start(bf16[384,512]{1,0:T(8,128)(2,1)S(1)} %get-tuple-element.88), channel_id=1, source_target_pairs={{0,8},{1,9},{2,10},{3,11},{4,12},{5,13},{6,14},{7,15},{8,0},{9,1},... | collective-permute-start | bytes 1179656 | tf_op jit(solution)/shard_map/ppermute | solution.py:47
  68.5 2.3 select_grad.1
  70.8 6.8 %collective-permute-done.11.refs_1_ = bf16[384,512]{1,0:T(8,128)(2,1)S(1)} collective-permute-done((bf16[384,512]{1,0:T(8,128)(2,1)S(1)}, bf16[384,512]{1,0:T(8,128)(2,1)S(1)}, u32[]{:S(2)}, u32[]{:S(2)}) %collective-permute-start.11) | collective-permute-done | bytes 393248 | tf_op jit(solution)/shard_map/ppermute | solution.py:47
  79.3 8.7 %collective-permute-start.6 = (bf16[384,512]{1,0:T(8,128)(2,1)S(1)}, bf16[384,512]{1,0:T(8,128)(2,1)S(1)}, u32[]{:S(2)}, u32[]{:S(2)}) collective-permute-start(bf16[384,512]{1,0:T(8,128)(2,1)S(1)} %get-tuple-element.79), channel_id=1, source_target_pairs={{0,8},{1,9},{2,10},{3,11},{4,12},{5,13},{6,14},{7,15},{8,0},{9,1},... | collective-permute-start | bytes 1179656 | tf_op jit(solution)/shard_map/ppermute | solution.py:47
  88.1 1.6 collective-permute-start.7
  89.8 6.2 %collective-permute-done.5.refs_1_ = bf16[384,512]{1,0:T(8,128)(2,1)S(1)} collective-permute-done((bf16[384,512]{1,0:T(8,128)(2,1)S(1)}, bf16[384,512]{1,0:T(8,128)(2,1)S(1)}, u32[]{:S(2)}, u32[]{:S(2)}) %collective-permute-start.5) | collective-permute-done | bytes 393248 | tf_op jit(solution)/shard_map/ppermute | solution.py:47
  96.0 1.5 collective-permute-start.14
  98.1 3.0 %collective-permute-start.15 = (bf16[384,512]{1,0:T(8,128)(2,1)S(1)}, bf16[384,512]{1,0:T(8,128)(2,1)S(1)}, u32[]{:S(2)}, u32[]{:S(2)}) collective-permute-start(bf16[384,512]{1,0:T(8,128)(2,1)S(1)} %get-tuple-element.92), channel_id=1, source_target_pairs={{0,2},{1,3},{2,0},{3,1},{4,6},{5,7},{6,4},{7,5},{8,10},{9,11},{10,... | collective-permute-start | bytes 1179656 | tf_op jit(solution)/shard_map/ppermute | solution.py:47
  101.1 3.0 %collective-permute-done.7.refs_3_ = bf16[384,512]{1,0:T(8,128)(2,1)S(1)} collective-permute-done((bf16[384,512]{1,0:T(8,128)(2,1)S(1)}, bf16[384,512]{1,0:T(8,128)(2,1)S(1)}, u32[]{:S(2)}, u32[]{:S(2)}) %collective-permute-start.7) | collective-permute-done | bytes 393248 | tf_op jit(solution)/shard_map/ppermute | solution.py:47
  104.0 2.8 %collective-permute-start.16 = (bf16[384,512]{1,0:T(8,128)(2,1)S(1)}, bf16[384,512]{1,0:T(8,128)(2,1)S(1)}, u32[]{:S(2)}, u32[]{:S(2)}) collective-permute-start(bf16[384,512]{1,0:T(8,128)(2,1)S(1)} %get-tuple-element.93), channel_id=1, source_target_pairs={{0,130},{1,131},{2,128},{3,129},{4,134},{5,135},{6,132},{7,133},{8... | collective-permute-start | bytes 1179656 | tf_op jit(solution)/shard_map/ppermute | solution.py:47
  108.0 1.5 collective-permute-start.8
  109.5 9.2 %collective-permute-done.15.refs_2_ = bf16[384,512]{1,0:T(8,128)(2,1)S(1)} collective-permute-done((bf16[384,512]{1,0:T(8,128)(2,1)S(1)}, bf16[384,512]{1,0:T(8,128)(2,1)S(1)}, u32[]{:S(2)}, u32[]{:S(2)}) %collective-permute-start.15) | collective-permute-done | bytes 393248 | tf_op jit(solution)/shard_map/ppermute | solution.py:47
  119.4 5.2 %collective-permute-done.16.refs_3_ = bf16[384,512]{1,0:T(8,128)(2,1)S(1)} collective-permute-done((bf16[384,512]{1,0:T(8,128)(2,1)S(1)}, bf16[384,512]{1,0:T(8,128)(2,1)S(1)}, u32[]{:S(2)}, u32[]{:S(2)}) %collective-permute-start.16) | collective-permute-done | bytes 393248 | tf_op jit(solution)/shard_map/ppermute | solution.py:47
  125.5 2.8 %collective-permute-start.10 = (bf16[384,512]{1,0:T(8,128)(2,1)S(1)}, bf16[384,512]{1,0:T(8,128)(2,1)S(1)}, u32[]{:S(2)}, u32[]{:S(2)}) collective-permute-start(bf16[384,512]{1,0:T(8,128)(2,1)S(1)} %get-tuple-element.84), channel_id=1, source_target_pairs={{0,130},{1,131},{2,128},{3,129},{4,134},{5,135},{6,132},{7,133},{8... | collective-permute-start | bytes 1179656 | tf_op jit(solution)/shard_map/ppermute | solution.py:47
  128.8 6.1 %expert_forward.1 = (f32[384,768]{1,0:T(8,128)S(1)}, f32[384,768]{1,0:T(8,128)S(1)}, bf16[384,768]{1,0:T(8,128)(2,1)S(1)}, bf16[384,64]{1,0:T(8,128)(2,1)S(1)}, ...) custom-call(s32[9]{0:T(128)S(1)} %stack.48.scalars, bf16[2,384,512]{2,1,0:T(8,128)(2,1)S(1)} %get-tuple-element.94.refs_0_.refs_2_, ...), custom_call_target="tpu_custom_call" | custom-call | tf_op jit(solution)/shard_map/expert_forward/pallas_call | solution.py:328
  134.9 6.3 %collective-permute-done.10.refs_3_ = bf16[384,512]{1,0:T(8,128)(2,1)S(1)} collective-permute-done((bf16[384,512]{1,0:T(8,128)(2,1)S(1)}, bf16[384,512]{1,0:T(8,128)(2,1)S(1)}, u32[]{:S(2)}, u32[]{:S(2)}) %collective-permute-start.10) | collective-permute-done | bytes 393248 | tf_op jit(solution)/shard_map/ppermute | solution.py:47
  142.1 2.2 collective-permute-done.21.refs_1_.refs_5_
  144.3 13.2 %expert_backward.1 = (bf16[2,384,512]{2,1,0:T(8,128)(2,1)S(1)}, bf16[2,384,512]{2,1,0:T(8,128)(2,1)S(1)}, f32[192,2048]{1,0:T(8,128)S(1)}, f32[192,768]{1,0:T(8,128)S(1)}) custom-call(s32[9]{0:T(128)S(1)} %stack.48.scalars, bf16[2,384,512]{2,1,0:T(8,128)(2,1)S(1)} %get-tuple-element.109.refs_0_.refs_4_, ...), custom_call_target="tpu_custom_call" | custom-call | tf_op jit(solution)/shard_map/expert_backward/pallas_call | solution.py:401
  157.7 2.2 collective-permute-done.22.crossed_ref
  160.9 1.7 collective-permute-start.24
  162.6 2.8 %collective-permute-start.25 = (bf16[384,512]{1,0:T(8,128)(2,1)S(1)}, bf16[384,512]{1,0:T(8,128)(2,1)S(1)}, u32[]{:S(2)}, u32[]{:S(2)}) collective-permute-start(bf16[384,512]{1,0:T(8,128)(2,1)S(1)} %get-tuple-element.124), channel_id=1, source_target_pairs={{0,130},{1,131},{2,128},{3,129},{4,134},{5,135},{6,132},{7,133},{8... | collective-permute-start | bytes 1179656 | tf_op jit(solution)/shard_map/ppermute | solution.py:47
  165.3 7.3 %collective-permute-done.23.refs_1_ = bf16[384,512]{1,0:T(8,128)(2,1)S(1)} collective-permute-done((bf16[384,512]{1,0:T(8,128)(2,1)S(1)}, bf16[384,512]{1,0:T(8,128)(2,1)S(1)}, u32[]{:S(2)}, u32[]{:S(2)}) %collective-permute-start.23) | collective-permute-done | bytes 393248 | tf_op jit(solution)/shard_map/ppermute | solution.py:47
  172.6 7.6 %collective-permute-done.24.refs_2_ = bf16[384,512]{1,0:T(8,128)(2,1)S(1)} collective-permute-done((bf16[384,512]{1,0:T(8,128)(2,1)S(1)}, bf16[384,512]{1,0:T(8,128)(2,1)S(1)}, u32[]{:S(2)}, u32[]{:S(2)}) %collective-permute-start.24) | collective-permute-done | bytes 393248 | tf_op jit(solution)/shard_map/ppermute | solution.py:47
  180.2 2.6 %collective-permute-done.25.refs_3_ = bf16[384,512]{1,0:T(8,128)(2,1)S(1)} collective-permute-done((bf16[384,512]{1,0:T(8,128)(2,1)S(1)}, bf16[384,512]{1,0:T(8,128)(2,1)S(1)}, u32[]{:S(2)}, u32[]{:S(2)}) %collective-permute-start.25) | collective-permute-done | bytes 393248 | tf_op jit(solution)/shard_map/ppermute | solution.py:47
  183.3 1.8 collective-permute-start.26
  185.1 4.0 %collective-permute-start.27 = (bf16[384,512]{1,0:T(8,128)(2,1)S(1)}, bf16[384,512]{1,0:T(8,128)(2,1)S(1)}, u32[]{:S(2)}, u32[]{:S(2)}) collective-permute-start(bf16[384,512]{1,0:T(8,128)(2,1)S(1)} %get-tuple-element.131), channel_id=1, source_target_pairs={{8,0},{9,1},{10,2},{11,3},{12,4},{13,5},{14,6},{15,7},{0,8},{1,9},... | collective-permute-start | bytes 1179656 | tf_op jit(solution)/shard_map/ppermute | solution.py:47
  189.1 8.3 %collective-permute-done.26.refs_3_ = bf16[384,512]{1,0:T(8,128)(2,1)S(1)} collective-permute-done((bf16[384,512]{1,0:T(8,128)(2,1)S(1)}, bf16[384,512]{1,0:T(8,128)(2,1)S(1)}, u32[]{:S(2)}, u32[]{:S(2)}) %collective-permute-start.26) | collective-permute-done | bytes 393248 | tf_op jit(solution)/shard_map/ppermute | solution.py:47
  197.4 9.6 %collective-permute-done.27.refs_4_ = bf16[384,512]{1,0:T(8,128)(2,1)S(1)} collective-permute-done((bf16[384,512]{1,0:T(8,128)(2,1)S(1)}, bf16[384,512]{1,0:T(8,128)(2,1)S(1)}, u32[]{:S(2)}, u32[]{:S(2)}) %collective-permute-start.27) | collective-permute-done | bytes 393248 | tf_op jit(solution)/shard_map/ppermute | solution.py:47
  208.0 5.9 %collective-permute-start.29 = (bf16[256,512]{1,0:T(8,128)(2,1)S(1)}, bf16[256,512]{1,0:T(8,128)(2,1)S(1)}, u32[]{:S(2)}, u32[]{:S(2)}) collective-permute-start(bf16[256,512]{1,0:T(8,128)(2,1)S(1)} %get-tuple-element.134), channel_id=1, source_target_pairs={{0,112},{1,113},{2,114},{3,115},{4,116},{5,117},{6,118},{7,119},{8... | collective-permute-start | bytes 786440 | tf_op jit(solution)/shard_map/ppermute | solution.py:47
  213.9 3.4 %collective-permute-start.31 = (bf16[128,512]{1,0:T(8,128)(2,1)S(1)}, bf16[128,512]{1,0:T(8,128)(2,1)S(1)}, u32[]{:S(2)}, u32[]{:S(2)}) collective-permute-start(bf16[128,512]{1,0:T(8,128)(2,1)S(1)} %get-tuple-element.136), channel_id=1, source_target_pairs={{0,64},{1,65},{2,66},{3,67},{4,68},{5,69},{6,70},{7,71},{8,72},{9,... | collective-permute-start | bytes 393224 | tf_op jit(solution)/shard_map/ppermute | solution.py:47
  217.3 7.6 %collective-permute-done.29 = bf16[256,512]{1,0:T(8,128)(2,1)S(1)} collective-permute-done((bf16[256,512]{1,0:T(8,128)(2,1)S(1)}, bf16[256,512]{1,0:T(8,128)(2,1)S(1)}, u32[]{:S(2)}, u32[]{:S(2)}) %collective-permute-start.29) | collective-permute-done | bytes 262176 | tf_op jit(solution)/shard_map/ppermute | solution.py:47
  224.9 1.9 collective-permute-done.30
  229.7 2.9 %collective-permute-start.33 = (bf16[128,512]{1,0:T(8,128)(2,1)}, bf16[128,512]{1,0:T(8,128)(2,1)S(1)}, u32[]{:S(2)}, u32[]{:S(2)}) collective-permute-start(bf16[128,512]{1,0:T(8,128)(2,1)} %get-tuple-element.165), channel_id=1, source_target_pairs={{0,32},{1,33},{2,34},{3,35},{4,36},{5,37},{6,38},{7,39},{8,40},{9,... | collective-permute-start | bytes 393224 | tf_op jit(solution)/shard_map/ppermute | solution.py:47
  232.6 3.2 %collective-permute-done.32 = bf16[128,512]{1,0:T(8,128)(2,1)S(1)} collective-permute-done((bf16[128,512]{1,0:T(8,128)(2,1)}, bf16[128,512]{1,0:T(8,128)(2,1)S(1)}, u32[]{:S(2)}, u32[]{:S(2)}) %collective-permute-start.32) | collective-permute-done | bytes 131104 | tf_op jit(solution)/shard_map/ppermute | solution.py:47
  235.9 2.8 %collective-permute-done.33 = bf16[128,512]{1,0:T(8,128)(2,1)S(1)} collective-permute-done((bf16[128,512]{1,0:T(8,128)(2,1)}, bf16[128,512]{1,0:T(8,128)(2,1)S(1)}, u32[]{:S(2)}, u32[]{:S(2)}) %collective-permute-start.33) | collective-permute-done | bytes 131104 | tf_op jit(solution)/shard_map/ppermute | solution.py:47
  239.4 2.3 collective-permute-done.35
  (102 shorter events, 19.8 us)
Async XLA Ops:
  3.7 4.7 %copy-start.15 = (s32[128,8]{0,1:T(8,128)S(1)}, s32[128,8]{0,1:T(8,128)}, u32[]{:S(2)}) copy-start(s32[128,8]{0,1:T(8,128)} %param.16) | copy-start | bytes 12292
  3.7 4.7 %copy-start.16 = (f32[128,8]{0,1:T(8,128)S(1)}, f32[128,8]{0,1:T(8,128)}, u32[]{:S(2)}) copy-start(f32[128,8]{0,1:T(8,128)} %param.15) | copy-start | bytes 12292
  3.7 4.7 %copy-start.10 = (bf16[128,512]{1,0:T(8,128)(2,1)S(1)}, bf16[128,512]{1,0:T(8,128)(2,1)}, u32[]{:S(2)}) copy-start(bf16[128,512]{1,0:T(8,128)(2,1)} %param.14) | copy-start | bytes 393220
  3.8 4.7 %copy-start.11 = (bf16[128,512]{1,0:T(8,128)(2,1)S(1)}, bf16[128,512]{1,0:T(8,128)(2,1)}, u32[]{:S(2)}) copy-start(bf16[128,512]{1,0:T(8,128)(2,1)} %param.13) | copy-start | bytes 393220
  5.4 60.3 %collective-permute-start.18 = (bf16[640,2048]{1,0:T(8,128)(2,1)}, bf16[640,2048]{1,0:T(8,128)(2,1)S(1)}, u32[]{:S(2)}, u32[]{:S(2)}) collective-permute-start(bf16[640,2048]{1,0:T(8,128)(2,1)} %pad_maximum_fusion), channel_id=1, source_target_pairs={{0,2},{1,3},{2,0},{3,1},{4,6},{5,7},{6,4},{7,5},{8,10},{9,11},{10,... | collective-permute-start | bytes 7864328 | tf_op jit(solution)/shard_map/ppermute | solution.py:47
  8.5 17.7 %collective-permute-start.1 = (bf16[264,512]{1,0:T(8,128)(2,1)S(1)}, bf16[264,512]{1,0:T(8,128)(2,1)S(1)}, u32[]{:S(2)}, u32[]{:S(2)}) collective-permute-start(bf16[264,512]{1,0:T(8,128)(2,1)S(1)} %maximum_maximum_fusion.2.refs_0_.refs_4_), channel_id=1, source_target_pairs={{0,96},{1,97},{2,98},{3,99},{4,100},{5,101},{6,102},{7,103},{8,104... | collective-permute-start | bytes 811016 | tf_op jit(solution)/shard_map/ppermute | solution.py:47
  14.8 15.1 %collective-permute-start = (bf16[264,512]{1,0:T(8,128)(2,1)S(1)}, bf16[264,512]{1,0:T(8,128)(2,1)S(1)}, u32[]{:S(2)}, u32[]{:S(2)}) collective-permute-start(bf16[264,512]{1,0:T(8,128)(2,1)S(1)} %maximum_maximum_fusion.2.refs_0_.refs_4_), channel_id=1, source_target_pairs={{0,32},{1,33},{2,34},{3,35},{4,36},{5,37},{6,38},{7,39},{8,40},{9,... | collective-permute-start | bytes 811016 | tf_op jit(solution)/shard_map/ppermute | solution.py:47
  31.0 23.5 %collective-permute-start.4 = (bf16[528,512]{1,0:T(8,128)(2,1)}, bf16[528,512]{1,0:T(8,128)(2,1)}, u32[]{:S(2)}, u32[]{:S(2)}) collective-permute-start(bf16[528,512]{1,0:T(8,128)(2,1)} %get-tuple-element.168), channel_id=1, source_target_pairs={{0,112},{1,113},{2,114},{3,115},{4,116},{5,117},{6,118},{7,119},{8... | collective-permute-start | bytes 1622024 | tf_op jit(solution)/shard_map/ppermute | solution.py:47
  31.4 26.3 %collective-permute-start.3 = (bf16[528,512]{1,0:T(8,128)(2,1)}, bf16[528,512]{1,0:T(8,128)(2,1)}, u32[]{:S(2)}, u32[]{:S(2)}) collective-permute-start(bf16[528,512]{1,0:T(8,128)(2,1)} %get-tuple-element.169), channel_id=1, source_target_pairs={{0,16},{1,17},{2,18},{3,19},{4,20},{5,21},{6,22},{7,23},{8,24},{9,... | collective-permute-start | bytes 1622024 | tf_op jit(solution)/shard_map/ppermute | solution.py:47
  33.1 21.5 %collective-permute-start.2 = (bf16[264,512]{1,0:T(8,128)(2,1)S(1)}, bf16[264,512]{1,0:T(8,128)(2,1)}, u32[]{:S(2)}, u32[]{:S(2)}) collective-permute-start(bf16[264,512]{1,0:T(8,128)(2,1)S(1)} %maximum_maximum_fusion.2.refs_0_.refs_4_), channel_id=1, source_target_pairs={{0,64},{1,65},{2,66},{3,67},{4,68},{5,69},{6,70},{7,71},{8,72},{9,... | collective-permute-start | bytes 811016 | tf_op jit(solution)/shard_map/ppermute | solution.py:47
  34.0 27.9 %copy-start.4 = (bf16[2,2048,192]{1,2,0:T(8,128)(2,1)S(1)}, bf16[2,2048,192]{1,2,0:T(8,128)(2,1)}, u32[]{:S(2)}) copy-start(bf16[2,2048,192]{1,2,0:T(8,128)(2,1)} %param.17) | copy-start | bytes 4718596
  65.0 60.5 %collective-permute-start.19 = (bf16[640,2048]{1,0:T(8,128)(2,1)S(1)}, bf16[640,2048]{1,0:T(8,128)(2,1)S(1)}, u32[]{:S(2)}, u32[]{:S(2)}) collective-permute-start(bf16[640,2048]{1,0:T(8,128)(2,1)S(1)} %pad_maximum_fusion.1), channel_id=1, source_target_pairs={{0,1},{1,0},{2,3},{3,2},{4,5},{5,4},{6,7},{7,6},{8,9},{9,8},{10,11... | collective-permute-start | bytes 7864328 | tf_op jit(solution)/shard_map/ppermute | solution.py:47
  65.7 63.0 %copy-start = (bf16[640,2048]{1,0:T(8,128)(2,1)}, bf16[640,2048]{1,0:T(8,128)(2,1)S(1)}, u32[]{:S(2)}) copy-start(bf16[640,2048]{1,0:T(8,128)(2,1)S(1)} %collective-permute-done.18.refs_3_.refs_7_.refs_12_.refs_16_) | copy-start | bytes 7864324
  65.7 62.8 %collective-permute-start.20 = (bf16[640,2048]{1,0:T(8,128)(2,1)S(1)}, bf16[640,2048]{1,0:T(8,128)(2,1)S(1)}, u32[]{:S(2)}, u32[]{:S(2)}) collective-permute-start(bf16[640,2048]{1,0:T(8,128)(2,1)S(1)} %collective-permute-done.18.refs_3_.refs_7_.refs_12_.refs_16_), channel_id=1, source_target_pairs={{0,1},{1,0},{2,3},{3,2},{4,5},{5,4},{6,7},{7,6},{8,9},{9,8},{10,11... | collective-permute-start | bytes 7864328 | tf_op jit(solution)/shard_map/ppermute | solution.py:47
  65.7 12.0 %collective-permute-start.11 = (bf16[384,512]{1,0:T(8,128)(2,1)S(1)}, bf16[384,512]{1,0:T(8,128)(2,1)S(1)}, u32[]{:S(2)}, u32[]{:S(2)}) collective-permute-start(bf16[384,512]{1,0:T(8,128)(2,1)S(1)} %get-tuple-element.87), channel_id=1, source_target_pairs={{0,4},{1,5},{2,6},{3,7},{4,8},{5,9},{6,10},{7,11},{8,12},{9,13},{1... | collective-permute-start | bytes 1179656 | tf_op jit(solution)/shard_map/ppermute | solution.py:47
  65.8 13.5 %collective-permute-start.12 = (bf16[384,512]{1,0:T(8,128)(2,1)S(1)}, bf16[384,512]{1,0:T(8,128)(2,1)S(1)}, u32[]{:S(2)}, u32[]{:S(2)}) collective-permute-start(bf16[384,512]{1,0:T(8,128)(2,1)S(1)} %get-tuple-element.88), channel_id=1, source_target_pairs={{0,8},{1,9},{2,10},{3,11},{4,12},{5,13},{6,14},{7,15},{8,0},{9,1},... | collective-permute-start | bytes 1179656 | tf_op jit(solution)/shard_map/ppermute | solution.py:47
  68.5 19.6 %collective-permute-start.13 = (bf16[384,512]{1,0:T(8,128)(2,1)S(1)}, bf16[384,512]{1,0:T(8,128)(2,1)S(1)}, u32[]{:S(2)}, u32[]{:S(2)}) collective-permute-start(bf16[384,512]{1,0:T(8,128)(2,1)S(1)} %get-tuple-element.89), channel_id=1, source_target_pairs={{0,12},{1,13},{2,14},{3,15},{4,0},{5,1},{6,2},{7,3},{8,4},{9,5},{1... | collective-permute-start | bytes 1179656 | tf_op jit(solution)/shard_map/ppermute | solution.py:47
  77.7 18.3 %collective-permute-start.5 = (bf16[384,512]{1,0:T(8,128)(2,1)S(1)}, bf16[384,512]{1,0:T(8,128)(2,1)S(1)}, u32[]{:S(2)}, u32[]{:S(2)}) collective-permute-start(bf16[384,512]{1,0:T(8,128)(2,1)S(1)} %get-tuple-element.78), channel_id=1, source_target_pairs={{0,4},{1,5},{2,6},{3,7},{4,8},{5,9},{6,10},{7,11},{8,12},{9,13},{1... | collective-permute-start | bytes 1179656 | tf_op jit(solution)/shard_map/ppermute | solution.py:47
  79.3 18.7 %collective-permute-start.6 = (bf16[384,512]{1,0:T(8,128)(2,1)S(1)}, bf16[384,512]{1,0:T(8,128)(2,1)S(1)}, u32[]{:S(2)}, u32[]{:S(2)}) collective-permute-start(bf16[384,512]{1,0:T(8,128)(2,1)S(1)} %get-tuple-element.79), channel_id=1, source_target_pairs={{0,8},{1,9},{2,10},{3,11},{4,12},{5,13},{6,14},{7,15},{8,0},{9,1},... | collective-permute-start | bytes 1179656 | tf_op jit(solution)/shard_map/ppermute | solution.py:47
  88.1 16.0 %collective-permute-start.7 = (bf16[384,512]{1,0:T(8,128)(2,1)S(1)}, bf16[384,512]{1,0:T(8,128)(2,1)S(1)}, u32[]{:S(2)}, u32[]{:S(2)}) collective-permute-start(bf16[384,512]{1,0:T(8,128)(2,1)S(1)} %get-tuple-element.80), channel_id=1, source_target_pairs={{0,12},{1,13},{2,14},{3,15},{4,0},{5,1},{6,2},{7,3},{8,4},{9,5},{1... | collective-permute-start | bytes 1179656 | tf_op jit(solution)/shard_map/ppermute | solution.py:47
  96.0 12.0 %collective-permute-start.14 = (bf16[384,512]{1,0:T(8,128)(2,1)S(1)}, bf16[384,512]{1,0:T(8,128)(2,1)S(1)}, u32[]{:S(2)}, u32[]{:S(2)}) collective-permute-start(bf16[384,512]{1,0:T(8,128)(2,1)S(1)} %get-tuple-element.91), channel_id=1, source_target_pairs={{0,128},{1,129},{2,130},{3,131},{4,132},{5,133},{6,134},{7,135},{8... | collective-permute-start | bytes 1179656 | tf_op jit(solution)/shard_map/ppermute | solution.py:47
  98.1 20.5 %collective-permute-start.15 = (bf16[384,512]{1,0:T(8,128)(2,1)S(1)}, bf16[384,512]{1,0:T(8,128)(2,1)S(1)}, u32[]{:S(2)}, u32[]{:S(2)}) collective-permute-start(bf16[384,512]{1,0:T(8,128)(2,1)S(1)} %get-tuple-element.92), channel_id=1, source_target_pairs={{0,2},{1,3},{2,0},{3,1},{4,6},{5,7},{6,4},{7,5},{8,10},{9,11},{10,... | collective-permute-start | bytes 1179656 | tf_op jit(solution)/shard_map/ppermute | solution.py:47
  104.0 20.6 %collective-permute-start.16 = (bf16[384,512]{1,0:T(8,128)(2,1)S(1)}, bf16[384,512]{1,0:T(8,128)(2,1)S(1)}, u32[]{:S(2)}, u32[]{:S(2)}) collective-permute-start(bf16[384,512]{1,0:T(8,128)(2,1)S(1)} %get-tuple-element.93), channel_id=1, source_target_pairs={{0,130},{1,131},{2,128},{3,129},{4,134},{5,135},{6,132},{7,133},{8... | collective-permute-start | bytes 1179656 | tf_op jit(solution)/shard_map/ppermute | solution.py:47
  108.0 27.0 %collective-permute-start.8 = (bf16[384,512]{1,0:T(8,128)(2,1)S(1)}, bf16[384,512]{1,0:T(8,128)(2,1)S(1)}, u32[]{:S(2)}, u32[]{:S(2)}) collective-permute-start(bf16[384,512]{1,0:T(8,128)(2,1)S(1)} %get-tuple-element.82), channel_id=1, source_target_pairs={{0,128},{1,129},{2,130},{3,131},{4,132},{5,133},{6,134},{7,135},{8... | collective-permute-start | bytes 1179656 | tf_op jit(solution)/shard_map/ppermute | solution.py:47
  118.6 16.3 %collective-permute-start.9 = (bf16[384,512]{1,0:T(8,128)(2,1)S(1)}, bf16[384,512]{1,0:T(8,128)(2,1)S(1)}, u32[]{:S(2)}, u32[]{:S(2)}) collective-permute-start(bf16[384,512]{1,0:T(8,128)(2,1)S(1)} %get-tuple-element.83), channel_id=1, source_target_pairs={{0,2},{1,3},{2,0},{3,1},{4,6},{5,7},{6,4},{7,5},{8,10},{9,11},{10,... | collective-permute-start | bytes 1179656 | tf_op jit(solution)/shard_map/ppermute | solution.py:47
  124.7 4.1 %copy-start.7 = (bf16[2,2048,64]{1,2,0:T(8,128)(2,1)S(1)}, bf16[2,2048,64]{1,2,0:T(8,128)(2,1)}, u32[]{:S(2)}) copy-start(bf16[2,2048,64]{1,2,0:T(8,128)(2,1)} %param.20) | copy-start | bytes 1572868
  124.7 4.1 %copy-start.8 = (bf16[2,2048,64]{1,2,0:T(8,128)(2,1)S(1)}, bf16[2,2048,64]{1,2,0:T(8,128)(2,1)}, u32[]{:S(2)}) copy-start(bf16[2,2048,64]{1,2,0:T(8,128)(2,1)} %param.22) | copy-start | bytes 1572868
  125.3 3.4 %collective-permute-start.17 = (bf16[2,384,512]{2,1,0:T(8,128)(2,1)S(1)}, bf16[2,384,512]{2,1,0:T(8,128)(2,1)S(1)}, u32[]{:S(2)}, u32[]{:S(2)}) collective-permute-start(bf16[2,384,512]{2,1,0:T(8,128)(2,1)S(1)} %get-tuple-element.95), channel_id=1, source_target_pairs={{0,1},{1,0},{2,3},{3,2},{4,5},{5,4},{6,7},{7,6},{8,9},{9,8},{10,11... | collective-permute-start | bytes 2359304 | tf_op jit(solution)/shard_map/ppermute | solution.py:47
  125.5 9.4 %copy-start.1 = (bf16[640,2048]{1,0:T(8,128)(2,1)}, bf16[640,2048]{1,0:T(8,128)(2,1)S(1)}, u32[]{:S(2)}) copy-start(bf16[640,2048]{1,0:T(8,128)(2,1)S(1)} %collective-permute-done.19.refs_4_.refs_8_.refs_13_.refs_17_) | copy-start | bytes 7864324
  125.5 15.7 %collective-permute-start.10 = (bf16[384,512]{1,0:T(8,128)(2,1)S(1)}, bf16[384,512]{1,0:T(8,128)(2,1)S(1)}, u32[]{:S(2)}, u32[]{:S(2)}) collective-permute-start(bf16[384,512]{1,0:T(8,128)(2,1)S(1)} %get-tuple-element.84), channel_id=1, source_target_pairs={{0,130},{1,131},{2,128},{3,129},{4,134},{5,135},{6,132},{7,133},{8... | collective-permute-start | bytes 1179656 | tf_op jit(solution)/shard_map/ppermute | solution.py:47
  128.5 6.4 %copy-start.2 = (bf16[640,2048]{1,0:T(8,128)(2,1)}, bf16[640,2048]{1,0:T(8,128)(2,1)S(1)}, u32[]{:S(2)}) copy-start(bf16[640,2048]{1,0:T(8,128)(2,1)S(1)} %collective-permute-done.20.refs_5_.refs_9_.refs_14_.refs_18_) | copy-start | bytes 7864324
  128.7 15.5 %copy-start.9 = (bf16[2,64,2048]{2,1,0:T(8,128)(2,1)S(1)}, bf16[2,64,2048]{2,1,0:T(8,128)(2,1)}, u32[]{:S(2)}) copy-start(bf16[2,64,2048]{2,1,0:T(8,128)(2,1)} %refs_10_.1) | copy-start | bytes 1572868
  134.9 9.4 %copy-start.6 = (bf16[2,192,2048]{2,1,0:T(8,128)(2,1)S(1)}, bf16[2,192,2048]{2,1,0:T(8,128)(2,1)}, u32[]{:S(2)}) copy-start(bf16[2,192,2048]{2,1,0:T(8,128)(2,1)} %refs_6_.1) | copy-start | bytes 4718596
  141.9 2.4 collective-permute-start.21
  157.5 2.4 collective-permute-start.22
  160.6 12.1 %collective-permute-start.23 = (bf16[384,512]{1,0:T(8,128)(2,1)S(1)}, bf16[384,512]{1,0:T(8,128)(2,1)S(1)}, u32[]{:S(2)}, u32[]{:S(2)}) collective-permute-start(bf16[384,512]{1,0:T(8,128)(2,1)S(1)} %get-tuple-element.122), channel_id=1, source_target_pairs={{0,128},{1,129},{2,130},{3,131},{4,132},{5,133},{6,134},{7,135},{8... | collective-permute-start | bytes 1179656 | tf_op jit(solution)/shard_map/ppermute | solution.py:47
  160.9 19.4 %collective-permute-start.24 = (bf16[384,512]{1,0:T(8,128)(2,1)S(1)}, bf16[384,512]{1,0:T(8,128)(2,1)S(1)}, u32[]{:S(2)}, u32[]{:S(2)}) collective-permute-start(bf16[384,512]{1,0:T(8,128)(2,1)S(1)} %get-tuple-element.123), channel_id=1, source_target_pairs={{0,2},{1,3},{2,0},{3,1},{4,6},{5,7},{6,4},{7,5},{8,10},{9,11},{10,... | collective-permute-start | bytes 1179656 | tf_op jit(solution)/shard_map/ppermute | solution.py:47
  162.6 20.2 %collective-permute-start.25 = (bf16[384,512]{1,0:T(8,128)(2,1)S(1)}, bf16[384,512]{1,0:T(8,128)(2,1)S(1)}, u32[]{:S(2)}, u32[]{:S(2)}) collective-permute-start(bf16[384,512]{1,0:T(8,128)(2,1)S(1)} %get-tuple-element.124), channel_id=1, source_target_pairs={{0,130},{1,131},{2,128},{3,129},{4,134},{5,135},{6,132},{7,133},{8... | collective-permute-start | bytes 1179656 | tf_op jit(solution)/shard_map/ppermute | solution.py:47
  183.1 43.8 %collective-permute-start.34 = (f32[192,1408]{1,0:T(8,128)S(1)}, f32[192,1408]{1,0:T(8,128)S(1)}, u32[]{:S(2)}, u32[]{:S(2)}) collective-permute-start(f32[192,1408]{1,0:T(8,128)S(1)} %pad_maximum_fusion.2), channel_id=1, source_target_pairs={{0,1},{1,0},{2,3},{3,2},{4,5},{5,4},{6,7},{7,6},{8,9},{9,8},{10,11... | collective-permute-start | bytes 3244040 | tf_op jit(solution)/shard_map/ppermute | solution.py:47
  183.3 14.0 %collective-permute-start.26 = (bf16[384,512]{1,0:T(8,128)(2,1)S(1)}, bf16[384,512]{1,0:T(8,128)(2,1)S(1)}, u32[]{:S(2)}, u32[]{:S(2)}) collective-permute-start(bf16[384,512]{1,0:T(8,128)(2,1)S(1)} %get-tuple-element.130), channel_id=1, source_target_pairs={{4,0},{5,1},{6,2},{7,3},{8,4},{9,5},{10,6},{11,7},{12,8},{13,9},{1... | collective-permute-start | bytes 1179656 | tf_op jit(solution)/shard_map/ppermute | solution.py:47
  185.1 21.9 %collective-permute-start.27 = (bf16[384,512]{1,0:T(8,128)(2,1)S(1)}, bf16[384,512]{1,0:T(8,128)(2,1)S(1)}, u32[]{:S(2)}, u32[]{:S(2)}) collective-permute-start(bf16[384,512]{1,0:T(8,128)(2,1)S(1)} %get-tuple-element.131), channel_id=1, source_target_pairs={{8,0},{9,1},{10,2},{11,3},{12,4},{13,5},{14,6},{15,7},{0,8},{1,9},... | collective-permute-start | bytes 1179656 | tf_op jit(solution)/shard_map/ppermute | solution.py:47
  189.1 17.9 %collective-permute-start.28 = (bf16[384,512]{1,0:T(8,128)(2,1)S(1)}, bf16[384,512]{1,0:T(8,128)(2,1)S(1)}, u32[]{:S(2)}, u32[]{:S(2)}) collective-permute-start(bf16[384,512]{1,0:T(8,128)(2,1)S(1)} %get-tuple-element.132), channel_id=1, source_target_pairs={{12,0},{13,1},{14,2},{15,3},{0,4},{1,5},{2,6},{3,7},{4,8},{5,9},{6... | collective-permute-start | bytes 1179656 | tf_op jit(solution)/shard_map/ppermute | solution.py:47
  208.0 16.9 %collective-permute-start.29 = (bf16[256,512]{1,0:T(8,128)(2,1)S(1)}, bf16[256,512]{1,0:T(8,128)(2,1)S(1)}, u32[]{:S(2)}, u32[]{:S(2)}) collective-permute-start(bf16[256,512]{1,0:T(8,128)(2,1)S(1)} %get-tuple-element.134), channel_id=1, source_target_pairs={{0,112},{1,113},{2,114},{3,115},{4,116},{5,117},{6,118},{7,119},{8... | collective-permute-start | bytes 786440 | tf_op jit(solution)/shard_map/ppermute | solution.py:47
  213.9 13.0 %collective-permute-start.30 = (bf16[256,512]{1,0:T(8,128)(2,1)S(1)}, bf16[256,512]{1,0:T(8,128)(2,1)S(1)}, u32[]{:S(2)}, u32[]{:S(2)}) collective-permute-start(bf16[256,512]{1,0:T(8,128)(2,1)S(1)} %get-tuple-element.135), channel_id=1, source_target_pairs={{0,16},{1,17},{2,18},{3,19},{4,20},{5,21},{6,22},{7,23},{8,24},{9,... | collective-permute-start | bytes 786440 | tf_op jit(solution)/shard_map/ppermute | solution.py:47
  213.9 18.7 %collective-permute-start.31 = (bf16[128,512]{1,0:T(8,128)(2,1)S(1)}, bf16[128,512]{1,0:T(8,128)(2,1)S(1)}, u32[]{:S(2)}, u32[]{:S(2)}) collective-permute-start(bf16[128,512]{1,0:T(8,128)(2,1)S(1)} %get-tuple-element.136), channel_id=1, source_target_pairs={{0,64},{1,65},{2,66},{3,67},{4,68},{5,69},{6,70},{7,71},{8,72},{9,... | collective-permute-start | bytes 393224 | tf_op jit(solution)/shard_map/ppermute | solution.py:47
  228.2 13.5 %collective-permute-start.35 = (f32[192,704]{1,0:T(8,128)}, f32[192,704]{1,0:T(8,128)S(1)}, u32[]{:S(2)}, u32[]{:S(2)}) collective-permute-start(f32[192,704]{1,0:T(8,128)} %pad_maximum_fusion.4), channel_id=1, source_target_pairs={{0,2},{1,3},{2,0},{3,1},{4,6},{5,7},{6,4},{7,5},{8,10},{9,11},{10,... | collective-permute-start | bytes 1622024 | tf_op jit(solution)/shard_map/ppermute | solution.py:47
  229.7 6.2 %collective-permute-start.32 = (bf16[128,512]{1,0:T(8,128)(2,1)}, bf16[128,512]{1,0:T(8,128)(2,1)S(1)}, u32[]{:S(2)}, u32[]{:S(2)}) collective-permute-start(bf16[128,512]{1,0:T(8,128)(2,1)} %get-tuple-element.164), channel_id=1, source_target_pairs={{0,96},{1,97},{2,98},{3,99},{4,100},{5,101},{6,102},{7,103},{8,104... | collective-permute-start | bytes 393224 | tf_op jit(solution)/shard_map/ppermute | solution.py:47
  229.7 8.9 %collective-permute-start.33 = (bf16[128,512]{1,0:T(8,128)(2,1)}, bf16[128,512]{1,0:T(8,128)(2,1)S(1)}, u32[]{:S(2)}, u32[]{:S(2)}) collective-permute-start(bf16[128,512]{1,0:T(8,128)(2,1)} %get-tuple-element.165), channel_id=1, source_target_pairs={{0,32},{1,33},{2,34},{3,35},{4,36},{5,37},{6,38},{7,39},{8,40},{9,... | collective-permute-start | bytes 393224 | tf_op jit(solution)/shard_map/ppermute | solution.py:47
  (5 other events, 7.3 us)
where the time goes:
time: 247 us; the launch traced here: 243 us
  waiting for transfers between devices  136 us (55%)
  starting transfers between devices  63 us (26%)
  Pallas kernels  29.2 us (12%)
  other arithmetic  7.87 us (3%)
  local copies, waits for them, and re-layouts  6.33 us (3%)
    ppermute x36, waiting for transfers between devices, move(): return lax.ppermute(x, AXES, perm)  136 us
    ppermute x36, starting transfers between devices, move(): return lax.ppermute(x, AXES, perm)  63 us
    pallas_call x1, Pallas kernels, expert_backward(): pl.pallas_call(backward_kernel, grid_spec=pltpu.PrefetchScalarGridSpec(nu...  13.2 us
    pallas_call x1, Pallas kernels, expert_forward(): pl.pallas_call(forward_kernel, grid_spec=pltpu.PrefetchScalarGridSpec(num...  6.13 us
  transfers between devices with their start and end apart: 36, of which 26 were waited for; matrix products, arithmetic and copies ran while one was open for 3% of the time, Pallas kernels for 6%

commit v1 on v0

--- a/solution.py
+++ b/solution.py
@@ -253,17 +253,16 @@
 
         @pl.when(scalars[5] == swapped)
         def _(swapped=swapped):
-            for i in range(2):
-                home[2 * i + swapped][...] = own_ref[i]
-                home[2 * i + 1 - swapped][...] = crossed_ref[i]
+            home[swapped][...] = own_ref[...]
+            home[1 - swapped][...] = crossed_ref[...]
 
 
 def join(scalars, own, crossed):
     return pl.pallas_call(
         join_kernel,
         in_specs=[SCALARS, VMEM, VMEM],
-        out_specs=[VMEM] * 4,
-        out_shape=[jax.ShapeDtypeStruct(own.shape[1:], bf16)] * 4,
+        out_specs=[VMEM] * 2,
+        out_shape=[jax.ShapeDtypeStruct(own.shape, bf16)] * 2,
         compiler_params=grant(8),
         name="join_cores",
     )(scalars, own, crossed)
@@ -344,7 +343,7 @@
     cots, parts, late_cots, downs, refs = refs[:2], refs[2:4], refs[4:6], refs[6:11], refs[11:]
     gates, ups, firsts, seconds, refs = refs[:4], refs[4:8], refs[8:10], refs[10], refs[11:]
     gate_ref, up_ref, hidden_ref, lora_gate_ref, lora_up_ref, down_lora_ref, *refs = refs
-    own_ref, cross_ref, feature_ref, by_hidden_ref, acc, left = refs
+    own_ref, cross_ref, feature_ref, by_hidden_ref, left, acc = refs
     step = pl.program_id(0)
     rank = seconds.shape[0] // 3
     units = seconds.shape[1]
@@ -375,16 +374,59 @@
 
     @pl.when(step >= 4)
     def _():
-        weights = stack((*gates, *ups, *firsts))
-        result = dot(left[...], weights, 1, 0).astype(bf16)
-        for k, ref in enumerate((own_ref, cross_ref)):
-
-            @pl.when(step % 2 == k)
-            def _(ref=ref):
-                ref[0] = result
-
-        feature_ref[: 2 * rank, :] = dot(left[:, 2 * units :], part_of(parts, step), 0, 0)
-        feature_ref[2 * rank :, :] = SCALE * dot(down_lora_ref[...], part_of(late_cots, step), 0, 0)
+        by_block(
+            step, parts, late_cots, gates, ups, firsts, left, down_lora_ref,
+            own_ref, cross_ref, feature_ref,
+        )
+
+
+def by_block(step, parts, cots, gates, ups, firsts, left, down_lora, own_ref, cross_ref, feature_ref):
+    rank = down_lora.shape[1]
+    result = dot(left[...], stack((*gates, *ups, *firsts)), 1, 0).astype(bf16)
+    for k, ref in enumerate((own_ref, cross_ref)):
+
+        @pl.when(step % 2 == k)
+        def _(ref=ref):
+            ref[...] = result
+
+    feature_ref[: 2 * rank, :] = dot(left[:, left.shape[1] - 2 * rank :], part_of(parts, step), 0, 0)
+    feature_ref[2 * rank :, :] = SCALE * dot(down_lora[...], part_of(cots, step), 0, 0)
+
+
+def rest_kernel(scalars, *refs):
+    parts, cots, gates, ups, firsts = refs[:2], refs[2:4], refs[4:8], refs[8:12], refs[12:14]
+    left, down_lora, *outs = refs[14:]
+    by_block(pl.program_id(0), parts, cots, gates, ups, firsts, left, down_lora, *outs)
+
+
+def expert_rest(scalars, cots, parts, gates, ups, firsts, left, down_lora):
+    rows, width = parts[0].shape[1:]
+    rank, units = down_lora.shape[1], left.shape[1] // 2 - down_lora.shape[1]
+    piece = units // 4
+    block = lambda g: g
+    specs = part_specs(rows, width, block) * 2
+    specs += weight_specs(4, piece, width, block, 0) + weight_specs(4, piece, width, block, 1)
+    specs += weight_specs(1, rank, width, block) * 2 + [whole(left.shape), whole(down_lora.shape)]
+    return pl.pallas_call(
+        rest_kernel,
+        grid_spec=pltpu.PrefetchScalarGridSpec(
+            num_scalar_prefetch=1,
+            grid=(2,),
+            in_specs=specs,
+            out_specs=[
+                whole((rows, width)),
+                whole((rows, width)),
+                pl.BlockSpec((3 * rank, width), lambda g, s: (0, g)),
+            ],
+        ),
+        out_shape=[
+            jax.ShapeDtypeStruct((rows, width), bf16),
+            jax.ShapeDtypeStruct((rows, width), bf16),
+            jax.ShapeDtypeStruct((3 * rank, 2 * width), f32),
+        ],
+        compiler_params=grant(28),
+        name="expert_rest",
+    )(scalars, *parts, *cots, *gates, *ups, *firsts, left, down_lora)
 
 
 def expert_backward(scalars, cots, parts, downs, down_second, gates, ups, firsts, seconds, saved):
@@ -392,7 +434,7 @@
     rank, units = seconds.shape[0] // 3, seconds.shape[1]
     piece = units // 4
     early = lambda g: jnp.minimum(g, 3)
-    late = lambda g: jnp.maximum(g - 4, 0)
+    late = lambda g: 2 + jnp.maximum(g - 4, 0)
     specs = part_specs(rows, width, early) + part_specs(rows, width, late) * 2
     specs += weight_specs(4, piece, width, early, 2) + weight_specs(1, rank, width, early)
     specs += weight_specs(4, piece, width, late, 0) + weight_specs(4, piece, width, late, 1)
@@ -402,24 +444,25 @@
         backward_kernel,
         grid_spec=pltpu.PrefetchScalarGridSpec(
             num_scalar_prefetch=1,
-            grid=(8,),
+            grid=(6,),
             in_specs=specs,
             out_specs=[
-                pl.BlockSpec((1, rows, width), lambda g, s: (late(g) // 2, 0, 0)),
-                pl.BlockSpec((1, rows, width), lambda g, s: (late(g) // 2, 0, 0)),
-                pl.BlockSpec((3 * rank, width), lambda g, s: (0, late(g))),
+                whole((rows, width)),
+                whole((rows, width)),
+                pl.BlockSpec((3 * rank, width), lambda g, s: (0, late(g) - 2)),
                 whole((3 * rank, units)),
+                whole((rows, 2 * units + 2 * rank)),
             ],
             scratch_shapes=[
                 pltpu.VMEM((rows, units + rank), f32),
-                pltpu.VMEM((rows, 2 * units + 2 * rank), bf16),
             ],
         ),
         out_shape=[
-            jax.ShapeDtypeStruct((2, rows, width), bf16),
-            jax.ShapeDtypeStruct((2, rows, width), bf16),
-            jax.ShapeDtypeStruct((3 * rank, 4 * width), f32),
+            jax.ShapeDtypeStruct((rows, width), bf16),
+            jax.ShapeDtypeStruct((rows, width), bf16),
+            jax.ShapeDtypeStruct((3 * rank, 2 * width), f32),
             jax.ShapeDtypeStruct((3 * rank, units), f32),
+            jax.ShapeDtypeStruct((rows, 2 * units + 2 * rank), bf16),
         ],
         compiler_params=grant(36),
         name="expert_backward",
@@ -521,16 +564,22 @@
     tied = lax.optimization_barrier((*grad_sent, *saved))
     grad_sent, saved = tied[:4], tied[4:]
     grad_parts = to_core(grad_sent)
-    own_grad, cross_grad, by_feature, by_hidden = expert_backward(
+    own_1, cross_1, feature_1, by_hidden, left = expert_backward(
         scalars, grad_parts, in_parts, downs, down_adapter_second, gates, ups, firsts, seconds, saved
     )
 
-    home = join(scalars, own_grad, move(cross_grad, CORE))
-    home = [home[0]] + [move(home[k], X_BY[k]) for k in range(1, 4)]
-
-    by_feature, by_hidden, *home = lax.optimization_barrier((by_feature, by_hidden, *home))
-
-    feature = [by_feature[:, k * width : (k + 1) * width] for k in range(4)]
+    own_0, cross_0, feature_0 = expert_rest(
+        scalars, grad_parts, in_parts, gates, ups, firsts, left, saved[-1]
+    )
+    home_2, home_3 = join(scalars, own_1, move(cross_1, CORE))
+    home_2, home_3 = move(home_2, X_BY[2]), move(home_3, X_BY[3])
+    home_0, home_1 = join(scalars, own_0, move(cross_0, CORE))
+    home = [home_0, move(home_1, X_BY[1]), home_2, home_3]
+    feature_0, feature_1, by_hidden, *home = lax.optimization_barrier(
+        (feature_0, feature_1, by_hidden, *home)
+    )
+
+    feature = [f[:, k * width : (k + 1) * width] for f in (feature_0, feature_1) for k in range(2)]
     mine = jnp.concatenate((feature[0], feature[2], by_hidden[:, : 2 * units]), axis=1)
     other = jnp.concatenate((feature[1], feature[3], by_hidden[:, 2 * units :]), axis=1)
     total = mine + move(other, CORE)

time: 247 us -> 248 us (level)
    pallas_call x0 -> x1, Pallas kernels: none -> 3.65 us  [expert_rest(): pl.pallas_call(rest_kernel, grid_spec=pltpu.PrefetchScalarGridSpec(num_sc...]
    pallas_call x1, Pallas kernels: 13.2 us -> 10.5 us  [expert_backward(): pl.pallas_call(backward_kernel, grid_spec=pltpu.PrefetchScalarGridSpec(nu...]
    ppermute x36 -> x37, waiting for transfers between devices: 136 us -> 134 us  [move(): return lax.ppermute(x, AXES, perm)]
    ppermute x36 -> x37, starting transfers between devices: 63 us -> 64 us  [move(): return lax.ppermute(x, AXES, perm)]
  transfers between devices with their start and end apart: 36 -> 37, of which waited for: 26 -> 26; matrix products, arithmetic and copies ran while one was open for 3% -> 3% of each run, Pallas kernels for 6% -> 6%
where the time goes in v1:
time: 248 us; the launch traced here: 245 us
  waiting for transfers between devices  134 us (54%)
  starting transfers between devices  64 us (26%)
  Pallas kernels  30.7 us (12%)
  other arithmetic  7.84 us (3%)
  local copies, waits for them, and re-layouts  6.57 us (3%)
    ppermute x37, waiting for transfers between devices, move(): return lax.ppermute(x, AXES, perm)  134 us
    ppermute x37, starting transfers between devices, move(): return lax.ppermute(x, AXES, perm)  64 us
    pallas_call x1, Pallas kernels, expert_backward(): pl.pallas_call(backward_kernel, grid_spec=pltpu.PrefetchScalarGridSpec(nu...  10.5 us
    pallas_call x1, Pallas kernels, expert_forward(): pl.pallas_call(forward_kernel, grid_spec=pltpu.PrefetchScalarGridSpec(num...  6.09 us
  transfers between devices with their start and end apart: 37, of which 26 were waited for; matrix products, arithmetic and copies ran while one was open for 3% of the time, Pallas kernels for 6%

profile of v1, /device:TPU:24, one launch (start us, length us, event | category | flops | bytes accessed | tf_op | source)
XLA Modules:
  0.0 244.8 jit_solution(8360588172085349148)
XLA Ops:
  0.7 1.3 dynamic-slice_bitcast_fusion.3
  3.8 1.6 pad_maximum_fusion
  5.4 3.0 %collective-permute-start.18 = (bf16[640,2048]{1,0:T(8,128)(2,1)}, bf16[640,2048]{1,0:T(8,128)(2,1)S(1)}, u32[]{:S(2)}, u32[]{:S(2)}) collective-permute-start(bf16[640,2048]{1,0:T(8,128)(2,1)} %pad_maximum_fusion), channel_id=1, source_target_pairs={{0,2},{1,3},{2,0},{3,1},{4,6},{5,7},{6,4},{7,5},{8,10},{9,11},{10,... | collective-permute-start | bytes 7864328 | tf_op jit(solution)/shard_map/ppermute | solution.py:47
  8.5 6.4 %collective-permute-start.1 = (bf16[264,512]{1,0:T(8,128)(2,1)S(1)}, bf16[264,512]{1,0:T(8,128)(2,1)S(1)}, u32[]{:S(2)}, u32[]{:S(2)}) collective-permute-start(bf16[264,512]{1,0:T(8,128)(2,1)S(1)} %maximum_maximum_fusion.2.refs_0_.refs_4_), channel_id=1, source_target_pairs={{0,96},{1,97},{2,98},{3,99},{4,100},{5,101},{6,102},{7,103},{8,104... | collective-permute-start | bytes 811016 | tf_op jit(solution)/shard_map/ppermute | solution.py:47
  14.9 11.3 %collective-permute-done.1.refs_2_.refs_6_ = bf16[264,512]{1,0:T(8,128)(2,1)S(1)} collective-permute-done((bf16[264,512]{1,0:T(8,128)(2,1)S(1)}, bf16[264,512]{1,0:T(8,128)(2,1)S(1)}, u32[]{:S(2)}, u32[]{:S(2)}) %collective-permute-start.1) | collective-permute-done | bytes 270368 | tf_op jit(solution)/shard_map/ppermute | solution.py:47
  26.2 3.8 %collective-permute-done.refs_1_.refs_5_ = bf16[264,512]{1,0:T(8,128)(2,1)S(1)} collective-permute-done((bf16[264,512]{1,0:T(8,128)(2,1)S(1)}, bf16[264,512]{1,0:T(8,128)(2,1)S(1)}, u32[]{:S(2)}, u32[]{:S(2)}) %collective-permute-start) | collective-permute-done | bytes 270368 | tf_op jit(solution)/shard_map/ppermute | solution.py:47
  31.5 1.7 collective-permute-start.3
  34.2 20.5 %collective-permute-done.2.refs_3_.refs_7_ = bf16[264,512]{1,0:T(8,128)(2,1)} collective-permute-done((bf16[264,512]{1,0:T(8,128)(2,1)S(1)}, bf16[264,512]{1,0:T(8,128)(2,1)}, u32[]{:S(2)}, u32[]{:S(2)}) %collective-permute-start.2) | collective-permute-done | bytes 270368 | tf_op jit(solution)/shard_map/ppermute | solution.py:47
  54.7 3.1 %collective-permute-done.3.refs_4_.refs_8_ = bf16[528,512]{1,0:T(8,128)(2,1)} collective-permute-done((bf16[528,512]{1,0:T(8,128)(2,1)}, bf16[528,512]{1,0:T(8,128)(2,1)}, u32[]{:S(2)}, u32[]{:S(2)}) %collective-permute-start.3) | collective-permute-done | bytes 540704 | tf_op jit(solution)/shard_map/ppermute | solution.py:47
  57.7 4.2 %select_in.1 = (bf16[768,512]{1,0:T(8,128)(2,1)S(1)}, bf16[768,512]{1,0:T(8,128)(2,1)S(1)}, f32[768,128]{1,0:T(8,128)S(1)}, f32[768,128]{1,0:T(8,128)S(1)}, bf16...) custom-call(s32[9]{0:T(128)S(1)} %stack.48.scalars, ...), custom_call_target="tpu_custom_call" | custom-call | tf_op jit(solution)/shard_map/select_in/pallas_call | solution.py:132
  62.1 1.6 copy-done.9
  63.7 1.3 dynamic-slice_bitcast_fusion
  66.1 2.6 %collective-permute-start.6 = (bf16[384,512]{1,0:T(8,128)(2,1)S(1)}, bf16[384,512]{1,0:T(8,128)(2,1)S(1)}, u32[]{:S(2)}, u32[]{:S(2)}) collective-permute-start(bf16[384,512]{1,0:T(8,128)(2,1)S(1)} %get-tuple-element.83), channel_id=1, source_target_pairs={{0,8},{1,9},{2,10},{3,11},{4,12},{5,13},{6,14},{7,15},{8,0},{9,1},... | collective-permute-start | bytes 1179656 | tf_op jit(solution)/shard_map/ppermute | solution.py:47
  68.7 2.3 select_grad.1
  71.0 6.8 %collective-permute-done.5.refs_1_ = bf16[384,512]{1,0:T(8,128)(2,1)S(1)} collective-permute-done((bf16[384,512]{1,0:T(8,128)(2,1)S(1)}, bf16[384,512]{1,0:T(8,128)(2,1)S(1)}, u32[]{:S(2)}, u32[]{:S(2)}) %collective-permute-start.5) | collective-permute-done | bytes 393248 | tf_op jit(solution)/shard_map/ppermute | solution.py:47
  79.6 8.4 %collective-permute-start.13 = (bf16[384,512]{1,0:T(8,128)(2,1)S(1)}, bf16[384,512]{1,0:T(8,128)(2,1)S(1)}, u32[]{:S(2)}, u32[]{:S(2)}) collective-permute-start(bf16[384,512]{1,0:T(8,128)(2,1)S(1)} %get-tuple-element.95), channel_id=1, source_target_pairs={{0,8},{1,9},{2,10},{3,11},{4,12},{5,13},{6,14},{7,15},{8,0},{9,1},... | collective-permute-start | bytes 1179656 | tf_op jit(solution)/shard_map/ppermute | solution.py:47
  88.0 1.9 collective-permute-start.14
  90.0 5.9 %collective-permute-done.12.refs_1_ = bf16[384,512]{1,0:T(8,128)(2,1)S(1)} collective-permute-done((bf16[384,512]{1,0:T(8,128)(2,1)S(1)}, bf16[384,512]{1,0:T(8,128)(2,1)S(1)}, u32[]{:S(2)}, u32[]{:S(2)}) %collective-permute-start.12) | collective-permute-done | bytes 393248 | tf_op jit(solution)/shard_map/ppermute | solution.py:47
  95.9 1.6 collective-permute-start.8
  98.0 3.2 %collective-permute-start.9 = (bf16[384,512]{1,0:T(8,128)(2,1)S(1)}, bf16[384,512]{1,0:T(8,128)(2,1)S(1)}, u32[]{:S(2)}, u32[]{:S(2)}) collective-permute-start(bf16[384,512]{1,0:T(8,128)(2,1)S(1)} %get-tuple-element.87), channel_id=1, source_target_pairs={{0,2},{1,3},{2,0},{3,1},{4,6},{5,7},{6,4},{7,5},{8,10},{9,11},{10,... | collective-permute-start | bytes 1179656 | tf_op jit(solution)/shard_map/ppermute | solution.py:47
  101.1 3.0 %collective-permute-done.14.refs_3_ = bf16[384,512]{1,0:T(8,128)(2,1)S(1)} collective-permute-done((bf16[384,512]{1,0:T(8,128)(2,1)S(1)}, bf16[384,512]{1,0:T(8,128)(2,1)S(1)}, u32[]{:S(2)}, u32[]{:S(2)}) %collective-permute-start.14) | collective-permute-done | bytes 393248 | tf_op jit(solution)/shard_map/ppermute | solution.py:47
  104.1 2.8 %collective-permute-start.10 = (bf16[384,512]{1,0:T(8,128)(2,1)S(1)}, bf16[384,512]{1,0:T(8,128)(2,1)S(1)}, u32[]{:S(2)}, u32[]{:S(2)}) collective-permute-start(bf16[384,512]{1,0:T(8,128)(2,1)S(1)} %get-tuple-element.88), channel_id=1, source_target_pairs={{0,130},{1,131},{2,128},{3,129},{4,134},{5,135},{6,132},{7,133},{8... | collective-permute-start | bytes 1179656 | tf_op jit(solution)/shard_map/ppermute | solution.py:47
  107.9 1.6 collective-permute-start.15
  109.5 9.2 %collective-permute-done.9.refs_2_ = bf16[384,512]{1,0:T(8,128)(2,1)S(1)} collective-permute-done((bf16[384,512]{1,0:T(8,128)(2,1)S(1)}, bf16[384,512]{1,0:T(8,128)(2,1)S(1)}, u32[]{:S(2)}, u32[]{:S(2)}) %collective-permute-start.9) | collective-permute-done | bytes 393248 | tf_op jit(solution)/shard_map/ppermute | solution.py:47
  119.5 5.2 %collective-permute-done.10.refs_3_ = bf16[384,512]{1,0:T(8,128)(2,1)S(1)} collective-permute-done((bf16[384,512]{1,0:T(8,128)(2,1)S(1)}, bf16[384,512]{1,0:T(8,128)(2,1)S(1)}, u32[]{:S(2)}, u32[]{:S(2)}) %collective-permute-start.10) | collective-permute-done | bytes 393248 | tf_op jit(solution)/shard_map/ppermute | solution.py:47
  125.6 2.7 %collective-permute-start.17 = (bf16[384,512]{1,0:T(8,128)(2,1)S(1)}, bf16[384,512]{1,0:T(8,128)(2,1)S(1)}, u32[]{:S(2)}, u32[]{:S(2)}) collective-permute-start(bf16[384,512]{1,0:T(8,128)(2,1)S(1)} %get-tuple-element.100), channel_id=1, source_target_pairs={{0,130},{1,131},{2,128},{3,129},{4,134},{5,135},{6,132},{7,133},{8... | collective-permute-start | bytes 1179656 | tf_op jit(solution)/shard_map/ppermute | solution.py:47
  128.7 6.1 %expert_forward.1 = (f32[384,768]{1,0:T(8,128)S(1)}, f32[384,768]{1,0:T(8,128)S(1)}, bf16[384,768]{1,0:T(8,128)(2,1)S(1)}, bf16[384,64]{1,0:T(8,128)(2,1)S(1)}, ...) custom-call(s32[9]{0:T(128)S(1)} %stack.48.scalars, bf16[2,384,512]{2,1,0:T(8,128)(2,1)S(1)} %get-tuple-element.89.refs_0_.refs_2_, ...), custom_call_target="tpu_custom_call" | custom-call | tf_op jit(solution)/shard_map/expert_forward/pallas_call | solution.py:327
  134.9 6.4 %collective-permute-done.17.refs_3_ = bf16[384,512]{1,0:T(8,128)(2,1)S(1)} collective-permute-done((bf16[384,512]{1,0:T(8,128)(2,1)S(1)}, bf16[384,512]{1,0:T(8,128)(2,1)S(1)}, u32[]{:S(2)}, u32[]{:S(2)}) %collective-permute-start.17) | collective-permute-done | bytes 393248 | tf_op jit(solution)/shard_map/ppermute | solution.py:47
  142.1 2.2 collective-permute-done.21.refs_1_.refs_5_.refs_3_
  144.4 10.5 %expert_backward.1 = (bf16[384,512]{1,0:T(8,128)(2,1)S(1)}, bf16[384,512]{1,0:T(8,128)(2,1)S(1)}, f32[192,1024]{1,0:T(8,128)S(1)}, f32[192,768]{1,0:T(8,128)S(1)}, bf16[384,1664]{1,0:T(8,128)(2,1)S(1)}) custom-call(s32[9]{0:T(128)S(1)} %stack.48.scalars, bf16[2,384,512]{2,1,0:T(8,128)(2,1)S(1)} %get-tuple-element.114.refs_0_.refs_4_.refs_2_, ...), custom_call_target="tpu_custom_call" | custom-call | tf_op jit(solution)/shard_map/expert_backward/pallas_call | solution.py:443
  155.0 3.7 %expert_rest.1 = (bf16[384,512]{1,0:T(8,128)(2,1)S(1)}, bf16[384,512]{1,0:T(8,128)(2,1)S(1)}, f32[192,1024]{1,0:T(8,128)S(1)}) custom-call(s32[9]{0:T(128)S(1)} %stack.48.scalars, bf16[2,384,512]{2,1,0:T(8,128)(2,1)S(1)} %get-tuple-element.89.refs_0_.refs_2_, bf16[2,384,512]{2,1,0:T(8,128)(2,1)S(1)} %collective-permute-done.11.refs_1_.refs_3_, ...), custom_call_target="tpu_custom_call" | custom-call | tf_op jit(solution)/shard_map/expert_rest/pallas_call | solution.py:410
  162.2 1.7 collective-permute-start.25
  163.9 2.9 %collective-permute-start.26 = (bf16[384,512]{1,0:T(8,128)(2,1)S(1)}, bf16[384,512]{1,0:T(8,128)(2,1)S(1)}, u32[]{:S(2)}, u32[]{:S(2)}) collective-permute-start(bf16[384,512]{1,0:T(8,128)(2,1)S(1)} %get-tuple-element.133), channel_id=1, source_target_pairs={{0,130},{1,131},{2,128},{3,129},{4,134},{5,135},{6,132},{7,133},{8... | collective-permute-start | bytes 1179656 | tf_op jit(solution)/shard_map/ppermute | solution.py:47
  166.7 6.6 %collective-permute-done.23.refs_1_ = bf16[384,512]{1,0:T(8,128)(2,1)S(1)} collective-permute-done((bf16[384,512]{1,0:T(8,128)(2,1)S(1)}, bf16[384,512]{1,0:T(8,128)(2,1)S(1)}, u32[]{:S(2)}, u32[]{:S(2)}) %collective-permute-start.23) | collective-permute-done | bytes 393248 | tf_op jit(solution)/shard_map/ppermute | solution.py:47
  173.3 7.5 %collective-permute-done.25.refs_2_ = bf16[384,512]{1,0:T(8,128)(2,1)S(1)} collective-permute-done((bf16[384,512]{1,0:T(8,128)(2,1)S(1)}, bf16[384,512]{1,0:T(8,128)(2,1)S(1)}, u32[]{:S(2)}, u32[]{:S(2)}) %collective-permute-start.25) | collective-permute-done | bytes 393248 | tf_op jit(solution)/shard_map/ppermute | solution.py:47
  180.8 3.3 %collective-permute-done.26.refs_3_ = bf16[384,512]{1,0:T(8,128)(2,1)S(1)} collective-permute-done((bf16[384,512]{1,0:T(8,128)(2,1)S(1)}, bf16[384,512]{1,0:T(8,128)(2,1)S(1)}, u32[]{:S(2)}, u32[]{:S(2)}) %collective-permute-start.26) | collective-permute-done | bytes 393248 | tf_op jit(solution)/shard_map/ppermute | solution.py:47
  184.6 1.9 collective-permute-start.27
  186.5 3.8 %collective-permute-start.28 = (bf16[384,512]{1,0:T(8,128)(2,1)S(1)}, bf16[384,512]{1,0:T(8,128)(2,1)S(1)}, u32[]{:S(2)}, u32[]{:S(2)}) collective-permute-start(bf16[384,512]{1,0:T(8,128)(2,1)S(1)} %get-tuple-element.140), channel_id=1, source_target_pairs={{8,0},{9,1},{10,2},{11,3},{12,4},{13,5},{14,6},{15,7},{0,8},{1,9},... | collective-permute-start | bytes 1179656 | tf_op jit(solution)/shard_map/ppermute | solution.py:47
  190.3 8.3 %collective-permute-done.27.refs_3_ = bf16[384,512]{1,0:T(8,128)(2,1)S(1)} collective-permute-done((bf16[384,512]{1,0:T(8,128)(2,1)S(1)}, bf16[384,512]{1,0:T(8,128)(2,1)S(1)}, u32[]{:S(2)}, u32[]{:S(2)}) %collective-permute-start.27) | collective-permute-done | bytes 393248 | tf_op jit(solution)/shard_map/ppermute | solution.py:47
  198.6 9.6 %collective-permute-done.28.refs_4_ = bf16[384,512]{1,0:T(8,128)(2,1)S(1)} collective-permute-done((bf16[384,512]{1,0:T(8,128)(2,1)S(1)}, bf16[384,512]{1,0:T(8,128)(2,1)S(1)}, u32[]{:S(2)}, u32[]{:S(2)}) %collective-permute-start.28) | collective-permute-done | bytes 393248 | tf_op jit(solution)/shard_map/ppermute | solution.py:47
  209.2 6.1 %collective-permute-start.30 = (bf16[256,512]{1,0:T(8,128)(2,1)S(1)}, bf16[256,512]{1,0:T(8,128)(2,1)S(1)}, u32[]{:S(2)}, u32[]{:S(2)}) collective-permute-start(bf16[256,512]{1,0:T(8,128)(2,1)S(1)} %get-tuple-element.143), channel_id=1, source_target_pairs={{0,112},{1,113},{2,114},{3,115},{4,116},{5,117},{6,118},{7,119},{8... | collective-permute-start | bytes 786440 | tf_op jit(solution)/shard_map/ppermute | solution.py:47
  215.3 3.4 %collective-permute-start.32 = (bf16[128,512]{1,0:T(8,128)(2,1)S(1)}, bf16[128,512]{1,0:T(8,128)(2,1)S(1)}, u32[]{:S(2)}, u32[]{:S(2)}) collective-permute-start(bf16[128,512]{1,0:T(8,128)(2,1)S(1)} %get-tuple-element.145), channel_id=1, source_target_pairs={{0,64},{1,65},{2,66},{3,67},{4,68},{5,69},{6,70},{7,71},{8,72},{9,... | collective-permute-start | bytes 393224 | tf_op jit(solution)/shard_map/ppermute | solution.py:47
  218.7 7.6 %collective-permute-done.30 = bf16[256,512]{1,0:T(8,128)(2,1)S(1)} collective-permute-done((bf16[256,512]{1,0:T(8,128)(2,1)S(1)}, bf16[256,512]{1,0:T(8,128)(2,1)S(1)}, u32[]{:S(2)}, u32[]{:S(2)}) %collective-permute-start.30) | collective-permute-done | bytes 262176 | tf_op jit(solution)/shard_map/ppermute | solution.py:47
  226.3 1.9 collective-permute-done.31
  231.0 2.9 %collective-permute-start.34 = (bf16[128,512]{1,0:T(8,128)(2,1)}, bf16[128,512]{1,0:T(8,128)(2,1)S(1)}, u32[]{:S(2)}, u32[]{:S(2)}) collective-permute-start(bf16[128,512]{1,0:T(8,128)(2,1)} %get-tuple-element.175), channel_id=1, source_target_pairs={{0,32},{1,33},{2,34},{3,35},{4,36},{5,37},{6,38},{7,39},{8,40},{9,... | collective-permute-start | bytes 393224 | tf_op jit(solution)/shard_map/ppermute | solution.py:47
  233.9 3.2 %collective-permute-done.33 = bf16[128,512]{1,0:T(8,128)(2,1)S(1)} collective-permute-done((bf16[128,512]{1,0:T(8,128)(2,1)}, bf16[128,512]{1,0:T(8,128)(2,1)S(1)}, u32[]{:S(2)}, u32[]{:S(2)}) %collective-permute-start.33) | collective-permute-done | bytes 131104 | tf_op jit(solution)/shard_map/ppermute | solution.py:47
  237.2 2.8 %collective-permute-done.34 = bf16[128,512]{1,0:T(8,128)(2,1)S(1)} collective-permute-done((bf16[128,512]{1,0:T(8,128)(2,1)}, bf16[128,512]{1,0:T(8,128)(2,1)S(1)}, u32[]{:S(2)}, u32[]{:S(2)}) %collective-permute-start.34) | collective-permute-done | bytes 131104 | tf_op jit(solution)/shard_map/ppermute | solution.py:47
  240.7 2.3 collective-permute-done.36
  (121 shorter events, 21.8 us)
Async XLA Ops:
  5.4 60.3 %collective-permute-start.18 = (bf16[640,2048]{1,0:T(8,128)(2,1)}, bf16[640,2048]{1,0:T(8,128)(2,1)S(1)}, u32[]{:S(2)}, u32[]{:S(2)}) collective-permute-start(bf16[640,2048]{1,0:T(8,128)(2,1)} %pad_maximum_fusion), channel_id=1, source_target_pairs={{0,2},{1,3},{2,0},{3,1},{4,6},{5,7},{6,4},{7,5},{8,10},{9,11},{10,... | collective-permute-start | bytes 7864328 | tf_op jit(solution)/shard_map/ppermute | solution.py:47
  8.5 17.7 %collective-permute-start.1 = (bf16[264,512]{1,0:T(8,128)(2,1)S(1)}, bf16[264,512]{1,0:T(8,128)(2,1)S(1)}, u32[]{:S(2)}, u32[]{:S(2)}) collective-permute-start(bf16[264,512]{1,0:T(8,128)(2,1)S(1)} %maximum_maximum_fusion.2.refs_0_.refs_4_), channel_id=1, source_target_pairs={{0,96},{1,97},{2,98},{3,99},{4,100},{5,101},{6,102},{7,103},{8,104... | collective-permute-start | bytes 811016 | tf_op jit(solution)/shard_map/ppermute | solution.py:47
  14.9 15.1 %collective-permute-start = (bf16[264,512]{1,0:T(8,128)(2,1)S(1)}, bf16[264,512]{1,0:T(8,128)(2,1)S(1)}, u32[]{:S(2)}, u32[]{:S(2)}) collective-permute-start(bf16[264,512]{1,0:T(8,128)(2,1)S(1)} %maximum_maximum_fusion.2.refs_0_.refs_4_), channel_id=1, source_target_pairs={{0,32},{1,33},{2,34},{3,35},{4,36},{5,37},{6,38},{7,39},{8,40},{9,... | collective-permute-start | bytes 811016 | tf_op jit(solution)/shard_map/ppermute | solution.py:47
  31.1 23.5 %collective-permute-start.4 = (bf16[528,512]{1,0:T(8,128)(2,1)}, bf16[528,512]{1,0:T(8,128)(2,1)}, u32[]{:S(2)}, u32[]{:S(2)}) collective-permute-start(bf16[528,512]{1,0:T(8,128)(2,1)} %get-tuple-element.178), channel_id=1, source_target_pairs={{0,112},{1,113},{2,114},{3,115},{4,116},{5,117},{6,118},{7,119},{8... | collective-permute-start | bytes 1622024 | tf_op jit(solution)/shard_map/ppermute | solution.py:47
  31.5 26.3 %collective-permute-start.3 = (bf16[528,512]{1,0:T(8,128)(2,1)}, bf16[528,512]{1,0:T(8,128)(2,1)}, u32[]{:S(2)}, u32[]{:S(2)}) collective-permute-start(bf16[528,512]{1,0:T(8,128)(2,1)} %get-tuple-element.179), channel_id=1, source_target_pairs={{0,16},{1,17},{2,18},{3,19},{4,20},{5,21},{6,22},{7,23},{8,24},{9,... | collective-permute-start | bytes 1622024 | tf_op jit(solution)/shard_map/ppermute | solution.py:47
  33.1 21.5 %collective-permute-start.2 = (bf16[264,512]{1,0:T(8,128)(2,1)S(1)}, bf16[264,512]{1,0:T(8,128)(2,1)}, u32[]{:S(2)}, u32[]{:S(2)}) collective-permute-start(bf16[264,512]{1,0:T(8,128)(2,1)S(1)} %maximum_maximum_fusion.2.refs_0_.refs_4_), channel_id=1, source_target_pairs={{0,64},{1,65},{2,66},{3,67},{4,68},{5,69},{6,70},{7,71},{8,72},{9,... | collective-permute-start | bytes 811016 | tf_op jit(solution)/shard_map/ppermute | solution.py:47
  34.1 27.9 %copy-start.7 = (bf16[2,2048,192]{1,2,0:T(8,128)(2,1)S(1)}, bf16[2,2048,192]{1,2,0:T(8,128)(2,1)}, u32[]{:S(2)}) copy-start(bf16[2,2048,192]{1,2,0:T(8,128)(2,1)} %param.17) | copy-start | bytes 4718596
  65.3 60.3 %collective-permute-start.19 = (bf16[640,2048]{1,0:T(8,128)(2,1)S(1)}, bf16[640,2048]{1,0:T(8,128)(2,1)S(1)}, u32[]{:S(2)}, u32[]{:S(2)}) collective-permute-start(bf16[640,2048]{1,0:T(8,128)(2,1)S(1)} %pad_maximum_fusion.1), channel_id=1, source_target_pairs={{0,1},{1,0},{2,3},{3,2},{4,5},{5,4},{6,7},{7,6},{8,9},{9,8},{10,11... | collective-permute-start | bytes 7864328 | tf_op jit(solution)/shard_map/ppermute | solution.py:47
  65.7 62.9 %copy-start = (bf16[640,2048]{1,0:T(8,128)(2,1)}, bf16[640,2048]{1,0:T(8,128)(2,1)S(1)}, u32[]{:S(2)}) copy-start(bf16[640,2048]{1,0:T(8,128)(2,1)S(1)} %collective-permute-done.18.refs_3_.refs_7_.refs_12_.refs_16_.refs_5_.refs_9_) | copy-start | bytes 7864324
  65.7 62.7 %collective-permute-start.20 = (bf16[640,2048]{1,0:T(8,128)(2,1)S(1)}, bf16[640,2048]{1,0:T(8,128)(2,1)S(1)}, u32[]{:S(2)}, u32[]{:S(2)}) collective-permute-start(bf16[640,2048]{1,0:T(8,128)(2,1)S(1)} %collective-permute-done.18.refs_3_.refs_7_.refs_12_.refs_16_.refs_5_.refs_9_), channel_id=1, source_target_pairs={{0,1},{1,0},{2,3},{3,2},{4,5},{5,4},{6,7},{7,6},{8,9},{9,8},{10,11... | collective-permute-start | bytes 7864328 | tf_op jit(solution)/shard_map/ppermute | solution.py:47
  65.9 12.0 %collective-permute-start.5 = (bf16[384,512]{1,0:T(8,128)(2,1)S(1)}, bf16[384,512]{1,0:T(8,128)(2,1)S(1)}, u32[]{:S(2)}, u32[]{:S(2)}) collective-permute-start(bf16[384,512]{1,0:T(8,128)(2,1)S(1)} %get-tuple-element.82), channel_id=1, source_target_pairs={{0,4},{1,5},{2,6},{3,7},{4,8},{5,9},{6,10},{7,11},{8,12},{9,13},{1... | collective-permute-start | bytes 1179656 | tf_op jit(solution)/shard_map/ppermute | solution.py:47
  66.1 13.5 %collective-permute-start.6 = (bf16[384,512]{1,0:T(8,128)(2,1)S(1)}, bf16[384,512]{1,0:T(8,128)(2,1)S(1)}, u32[]{:S(2)}, u32[]{:S(2)}) collective-permute-start(bf16[384,512]{1,0:T(8,128)(2,1)S(1)} %get-tuple-element.83), channel_id=1, source_target_pairs={{0,8},{1,9},{2,10},{3,11},{4,12},{5,13},{6,14},{7,15},{8,0},{9,1},... | collective-permute-start | bytes 1179656 | tf_op jit(solution)/shard_map/ppermute | solution.py:47
  68.7 19.3 %collective-permute-start.7 = (bf16[384,512]{1,0:T(8,128)(2,1)S(1)}, bf16[384,512]{1,0:T(8,128)(2,1)S(1)}, u32[]{:S(2)}, u32[]{:S(2)}) collective-permute-start(bf16[384,512]{1,0:T(8,128)(2,1)S(1)} %get-tuple-element.84), channel_id=1, source_target_pairs={{0,12},{1,13},{2,14},{3,15},{4,0},{5,1},{6,2},{7,3},{8,4},{9,5},{1... | collective-permute-start | bytes 1179656 | tf_op jit(solution)/shard_map/ppermute | solution.py:47
  77.9 18.0 %collective-permute-start.12 = (bf16[384,512]{1,0:T(8,128)(2,1)S(1)}, bf16[384,512]{1,0:T(8,128)(2,1)S(1)}, u32[]{:S(2)}, u32[]{:S(2)}) collective-permute-start(bf16[384,512]{1,0:T(8,128)(2,1)S(1)} %get-tuple-element.94), channel_id=1, source_target_pairs={{0,4},{1,5},{2,6},{3,7},{4,8},{5,9},{6,10},{7,11},{8,12},{9,13},{1... | collective-permute-start | bytes 1179656 | tf_op jit(solution)/shard_map/ppermute | solution.py:47
  79.6 18.3 %collective-permute-start.13 = (bf16[384,512]{1,0:T(8,128)(2,1)S(1)}, bf16[384,512]{1,0:T(8,128)(2,1)S(1)}, u32[]{:S(2)}, u32[]{:S(2)}) collective-permute-start(bf16[384,512]{1,0:T(8,128)(2,1)S(1)} %get-tuple-element.95), channel_id=1, source_target_pairs={{0,8},{1,9},{2,10},{3,11},{4,12},{5,13},{6,14},{7,15},{8,0},{9,1},... | collective-permute-start | bytes 1179656 | tf_op jit(solution)/shard_map/ppermute | solution.py:47
  88.0 16.1 %collective-permute-start.14 = (bf16[384,512]{1,0:T(8,128)(2,1)S(1)}, bf16[384,512]{1,0:T(8,128)(2,1)S(1)}, u32[]{:S(2)}, u32[]{:S(2)}) collective-permute-start(bf16[384,512]{1,0:T(8,128)(2,1)S(1)} %get-tuple-element.96), channel_id=1, source_target_pairs={{0,12},{1,13},{2,14},{3,15},{4,0},{5,1},{6,2},{7,3},{8,4},{9,5},{1... | collective-permute-start | bytes 1179656 | tf_op jit(solution)/shard_map/ppermute | solution.py:47
  95.9 12.0 %collective-permute-start.8 = (bf16[384,512]{1,0:T(8,128)(2,1)S(1)}, bf16[384,512]{1,0:T(8,128)(2,1)S(1)}, u32[]{:S(2)}, u32[]{:S(2)}) collective-permute-start(bf16[384,512]{1,0:T(8,128)(2,1)S(1)} %get-tuple-element.86), channel_id=1, source_target_pairs={{0,128},{1,129},{2,130},{3,131},{4,132},{5,133},{6,134},{7,135},{8... | collective-permute-start | bytes 1179656 | tf_op jit(solution)/shard_map/ppermute | solution.py:47
  98.0 20.7 %collective-permute-start.9 = (bf16[384,512]{1,0:T(8,128)(2,1)S(1)}, bf16[384,512]{1,0:T(8,128)(2,1)S(1)}, u32[]{:S(2)}, u32[]{:S(2)}) collective-permute-start(bf16[384,512]{1,0:T(8,128)(2,1)S(1)} %get-tuple-element.87), channel_id=1, source_target_pairs={{0,2},{1,3},{2,0},{3,1},{4,6},{5,7},{6,4},{7,5},{8,10},{9,11},{10,... | collective-permute-start | bytes 1179656 | tf_op jit(solution)/shard_map/ppermute | solution.py:47
  104.1 20.6 %collective-permute-start.10 = (bf16[384,512]{1,0:T(8,128)(2,1)S(1)}, bf16[384,512]{1,0:T(8,128)(2,1)S(1)}, u32[]{:S(2)}, u32[]{:S(2)}) collective-permute-start(bf16[384,512]{1,0:T(8,128)(2,1)S(1)} %get-tuple-element.88), channel_id=1, source_target_pairs={{0,130},{1,131},{2,128},{3,129},{4,134},{5,135},{6,132},{7,133},{8... | collective-permute-start | bytes 1179656 | tf_op jit(solution)/shard_map/ppermute | solution.py:47
  107.9 27.0 %collective-permute-start.15 = (bf16[384,512]{1,0:T(8,128)(2,1)S(1)}, bf16[384,512]{1,0:T(8,128)(2,1)S(1)}, u32[]{:S(2)}, u32[]{:S(2)}) collective-permute-start(bf16[384,512]{1,0:T(8,128)(2,1)S(1)} %get-tuple-element.98), channel_id=1, source_target_pairs={{0,128},{1,129},{2,130},{3,131},{4,132},{5,133},{6,134},{7,135},{8... | collective-permute-start | bytes 1179656 | tf_op jit(solution)/shard_map/ppermute | solution.py:47
  118.7 16.2 %collective-permute-start.16 = (bf16[384,512]{1,0:T(8,128)(2,1)S(1)}, bf16[384,512]{1,0:T(8,128)(2,1)S(1)}, u32[]{:S(2)}, u32[]{:S(2)}) collective-permute-start(bf16[384,512]{1,0:T(8,128)(2,1)S(1)} %get-tuple-element.99), channel_id=1, source_target_pairs={{0,2},{1,3},{2,0},{3,1},{4,6},{5,7},{6,4},{7,5},{8,10},{9,11},{10,... | collective-permute-start | bytes 1179656 | tf_op jit(solution)/shard_map/ppermute | solution.py:47
  125.4 3.2 %collective-permute-start.11 = (bf16[2,384,512]{2,1,0:T(8,128)(2,1)S(1)}, bf16[2,384,512]{2,1,0:T(8,128)(2,1)S(1)}, u32[]{:S(2)}, u32[]{:S(2)}) collective-permute-start(bf16[2,384,512]{2,1,0:T(8,128)(2,1)S(1)} %get-tuple-element.90), channel_id=1, source_target_pairs={{0,1},{1,0},{2,3},{3,2},{4,5},{5,4},{6,7},{7,6},{8,9},{9,8},{10,11... | collective-permute-start | bytes 2359304 | tf_op jit(solution)/shard_map/ppermute | solution.py:47
  125.6 9.2 %copy-start.2 = (bf16[640,2048]{1,0:T(8,128)(2,1)}, bf16[640,2048]{1,0:T(8,128)(2,1)S(1)}, u32[]{:S(2)}) copy-start(bf16[640,2048]{1,0:T(8,128)(2,1)S(1)} %collective-permute-done.19.refs_4_.refs_8_.refs_13_.refs_17_.refs_6_.refs_10_) | copy-start | bytes 7864324
  125.6 15.7 %collective-permute-start.17 = (bf16[384,512]{1,0:T(8,128)(2,1)S(1)}, bf16[384,512]{1,0:T(8,128)(2,1)S(1)}, u32[]{:S(2)}, u32[]{:S(2)}) collective-permute-start(bf16[384,512]{1,0:T(8,128)(2,1)S(1)} %get-tuple-element.100), channel_id=1, source_target_pairs={{0,130},{1,131},{2,128},{3,129},{4,134},{5,135},{6,132},{7,133},{8... | collective-permute-start | bytes 1179656 | tf_op jit(solution)/shard_map/ppermute | solution.py:47
  128.7 15.7 %copy-start.10 = (bf16[2,2048,192]{1,2,0:T(8,128)(2,1)S(1)}, bf16[2,2048,192]{1,2,0:T(8,128)(2,1)}, u32[]{:S(2)}) copy-start(bf16[2,2048,192]{1,2,0:T(8,128)(2,1)} %param.18) | copy-start | bytes 4718596
  128.7 15.7 %copy-start.11 = (bf16[2,192,2048]{2,1,0:T(8,128)(2,1)S(1)}, bf16[2,192,2048]{2,1,0:T(8,128)(2,1)}, u32[]{:S(2)}) copy-start(bf16[2,192,2048]{2,1,0:T(8,128)(2,1)} %refs_6_.1) | copy-start | bytes 4718596
  128.7 15.7 %copy-start.16 = (bf16[2,64,2048]{2,1,0:T(8,128)(2,1)S(1)}, bf16[2,64,2048]{2,1,0:T(8,128)(2,1)}, u32[]{:S(2)}) copy-start(bf16[2,64,2048]{2,1,0:T(8,128)(2,1)} %refs_10_.1) | copy-start | bytes 1572868
  134.8 9.5 %copy-start.8 = (bf16[2,2048,192]{1,2,0:T(8,128)(2,1)S(1)}, bf16[2,2048,192]{1,2,0:T(8,128)(2,1)}, u32[]{:S(2)}) copy-start(bf16[2,2048,192]{1,2,0:T(8,128)(2,1)} %param.17) | copy-start | bytes 4718596
  142.0 2.4 collective-permute-start.21
  144.4 10.6 %copy-start.1 = (bf16[640,2048]{1,0:T(8,128)(2,1)S(1)}, bf16[640,2048]{1,0:T(8,128)(2,1)}, u32[]{:S(2)}) copy-start(bf16[640,2048]{1,0:T(8,128)(2,1)} %copy-done) | copy-start | bytes 7864324
  144.4 10.6 %copy-start.3 = (bf16[640,2048]{1,0:T(8,128)(2,1)S(1)}, bf16[640,2048]{1,0:T(8,128)(2,1)}, u32[]{:S(2)}) copy-start(bf16[640,2048]{1,0:T(8,128)(2,1)} %copy-done.2) | copy-start | bytes 7864324
  144.4 10.6 %copy-start.5 = (bf16[640,2048]{1,0:T(8,128)(2,1)S(1)}, bf16[640,2048]{1,0:T(8,128)(2,1)}, u32[]{:S(2)}) copy-start(bf16[640,2048]{1,0:T(8,128)(2,1)} %copy-done.4) | copy-start | bytes 7864324
  158.6 1.8 collective-permute-start.22
  158.8 2.7 %collective-permute-start.24 = (bf16[384,512]{1,0:T(8,128)(2,1)S(1)}, bf16[384,512]{1,0:T(8,128)(2,1)S(1)}, u32[]{:S(2)}, u32[]{:S(2)}) collective-permute-start(bf16[384,512]{1,0:T(8,128)(2,1)S(1)} %get-tuple-element.131), channel_id=1, source_target_pairs={{0,1},{1,0},{2,3},{3,2},{4,5},{5,4},{6,7},{7,6},{8,9},{9,8},{10,11... | collective-permute-start | bytes 1179656 | tf_op jit(solution)/shard_map/ppermute | solution.py:47
  161.0 12.3 %collective-permute-start.23 = (bf16[384,512]{1,0:T(8,128)(2,1)S(1)}, bf16[384,512]{1,0:T(8,128)(2,1)S(1)}, u32[]{:S(2)}, u32[]{:S(2)}) collective-permute-start(bf16[384,512]{1,0:T(8,128)(2,1)S(1)} %get-tuple-element.129), channel_id=1, source_target_pairs={{0,128},{1,129},{2,130},{3,131},{4,132},{5,133},{6,134},{7,135},{8... | collective-permute-start | bytes 1179656 | tf_op jit(solution)/shard_map/ppermute | solution.py:47
  162.2 18.6 %collective-permute-start.25 = (bf16[384,512]{1,0:T(8,128)(2,1)S(1)}, bf16[384,512]{1,0:T(8,128)(2,1)S(1)}, u32[]{:S(2)}, u32[]{:S(2)}) collective-permute-start(bf16[384,512]{1,0:T(8,128)(2,1)S(1)} %get-tuple-element.132), channel_id=1, source_target_pairs={{0,2},{1,3},{2,0},{3,1},{4,6},{5,7},{6,4},{7,5},{8,10},{9,11},{10,... | collective-permute-start | bytes 1179656 | tf_op jit(solution)/shard_map/ppermute | solution.py:47
  163.9 20.3 %collective-permute-start.26 = (bf16[384,512]{1,0:T(8,128)(2,1)S(1)}, bf16[384,512]{1,0:T(8,128)(2,1)S(1)}, u32[]{:S(2)}, u32[]{:S(2)}) collective-permute-start(bf16[384,512]{1,0:T(8,128)(2,1)S(1)} %get-tuple-element.133), channel_id=1, source_target_pairs={{0,130},{1,131},{2,128},{3,129},{4,134},{5,135},{6,132},{7,133},{8... | collective-permute-start | bytes 1179656 | tf_op jit(solution)/shard_map/ppermute | solution.py:47
  184.4 23.9 %copy-start.15 = (bf16[768,512]{1,0:T(8,128)(2,1)S(1)}, bf16[768,512]{1,0:T(8,128)(2,1)}, u32[]{:S(2)}) copy-start(bf16[768,512]{1,0:T(8,128)(2,1)} %copy-done.14) | copy-start | bytes 2359300
  184.4 44.0 %collective-permute-start.35 = (f32[192,1408]{1,0:T(8,128)S(1)}, f32[192,1408]{1,0:T(8,128)S(1)}, u32[]{:S(2)}, u32[]{:S(2)}) collective-permute-start(f32[192,1408]{1,0:T(8,128)S(1)} %pad_maximum_fusion.2), channel_id=1, source_target_pairs={{0,1},{1,0},{2,3},{3,2},{4,5},{5,4},{6,7},{7,6},{8,9},{9,8},{10,11... | collective-permute-start | bytes 3244040 | tf_op jit(solution)/shard_map/ppermute | solution.py:47
  184.6 14.0 %collective-permute-start.27 = (bf16[384,512]{1,0:T(8,128)(2,1)S(1)}, bf16[384,512]{1,0:T(8,128)(2,1)S(1)}, u32[]{:S(2)}, u32[]{:S(2)}) collective-permute-start(bf16[384,512]{1,0:T(8,128)(2,1)S(1)} %get-tuple-element.139), channel_id=1, source_target_pairs={{4,0},{5,1},{6,2},{7,3},{8,4},{9,5},{10,6},{11,7},{12,8},{13,9},{1... | collective-permute-start | bytes 1179656 | tf_op jit(solution)/shard_map/ppermute | solution.py:47
  186.5 21.7 %collective-permute-start.28 = (bf16[384,512]{1,0:T(8,128)(2,1)S(1)}, bf16[384,512]{1,0:T(8,128)(2,1)S(1)}, u32[]{:S(2)}, u32[]{:S(2)}) collective-permute-start(bf16[384,512]{1,0:T(8,128)(2,1)S(1)} %get-tuple-element.140), channel_id=1, source_target_pairs={{8,0},{9,1},{10,2},{11,3},{12,4},{13,5},{14,6},{15,7},{0,8},{1,9},... | collective-permute-start | bytes 1179656 | tf_op jit(solution)/shard_map/ppermute | solution.py:47
  190.3 17.9 %collective-permute-start.29 = (bf16[384,512]{1,0:T(8,128)(2,1)S(1)}, bf16[384,512]{1,0:T(8,128)(2,1)S(1)}, u32[]{:S(2)}, u32[]{:S(2)}) collective-permute-start(bf16[384,512]{1,0:T(8,128)(2,1)S(1)} %get-tuple-element.141), channel_id=1, source_target_pairs={{12,0},{13,1},{14,2},{15,3},{0,4},{1,5},{2,6},{3,7},{4,8},{5,9},{6... | collective-permute-start | bytes 1179656 | tf_op jit(solution)/shard_map/ppermute | solution.py:47
  209.2 17.1 %collective-permute-start.30 = (bf16[256,512]{1,0:T(8,128)(2,1)S(1)}, bf16[256,512]{1,0:T(8,128)(2,1)S(1)}, u32[]{:S(2)}, u32[]{:S(2)}) collective-permute-start(bf16[256,512]{1,0:T(8,128)(2,1)S(1)} %get-tuple-element.143), channel_id=1, source_target_pairs={{0,112},{1,113},{2,114},{3,115},{4,116},{5,117},{6,118},{7,119},{8... | collective-permute-start | bytes 786440 | tf_op jit(solution)/shard_map/ppermute | solution.py:47
  215.3 13.0 %collective-permute-start.31 = (bf16[256,512]{1,0:T(8,128)(2,1)S(1)}, bf16[256,512]{1,0:T(8,128)(2,1)S(1)}, u32[]{:S(2)}, u32[]{:S(2)}) collective-permute-start(bf16[256,512]{1,0:T(8,128)(2,1)S(1)} %get-tuple-element.144), channel_id=1, source_target_pairs={{0,16},{1,17},{2,18},{3,19},{4,20},{5,21},{6,22},{7,23},{8,24},{9,... | collective-permute-start | bytes 786440 | tf_op jit(solution)/shard_map/ppermute | solution.py:47
  215.3 18.6 %collective-permute-start.32 = (bf16[128,512]{1,0:T(8,128)(2,1)S(1)}, bf16[128,512]{1,0:T(8,128)(2,1)S(1)}, u32[]{:S(2)}, u32[]{:S(2)}) collective-permute-start(bf16[128,512]{1,0:T(8,128)(2,1)S(1)} %get-tuple-element.145), channel_id=1, source_target_pairs={{0,64},{1,65},{2,66},{3,67},{4,68},{5,69},{6,70},{7,71},{8,72},{9,... | collective-permute-start | bytes 393224 | tf_op jit(solution)/shard_map/ppermute | solution.py:47
  229.5 13.5 %collective-permute-start.36 = (f32[192,704]{1,0:T(8,128)}, f32[192,704]{1,0:T(8,128)S(1)}, u32[]{:S(2)}, u32[]{:S(2)}) collective-permute-start(f32[192,704]{1,0:T(8,128)} %pad_maximum_fusion.4), channel_id=1, source_target_pairs={{0,2},{1,3},{2,0},{3,1},{4,6},{5,7},{6,4},{7,5},{8,10},{9,11},{10,... | collective-permute-start | bytes 1622024 | tf_op jit(solution)/shard_map/ppermute | solution.py:47
  231.0 6.2 %collective-permute-start.33 = (bf16[128,512]{1,0:T(8,128)(2,1)}, bf16[128,512]{1,0:T(8,128)(2,1)S(1)}, u32[]{:S(2)}, u32[]{:S(2)}) collective-permute-start(bf16[128,512]{1,0:T(8,128)(2,1)} %get-tuple-element.174), channel_id=1, source_target_pairs={{0,96},{1,97},{2,98},{3,99},{4,100},{5,101},{6,102},{7,103},{8,104... | collective-permute-start | bytes 393224 | tf_op jit(solution)/shard_map/ppermute | solution.py:47
  231.0 9.0 %collective-permute-start.34 = (bf16[128,512]{1,0:T(8,128)(2,1)}, bf16[128,512]{1,0:T(8,128)(2,1)S(1)}, u32[]{:S(2)}, u32[]{:S(2)}) collective-permute-start(bf16[128,512]{1,0:T(8,128)(2,1)} %get-tuple-element.175), channel_id=1, source_target_pairs={{0,32},{1,33},{2,34},{3,35},{4,36},{5,37},{6,38},{7,39},{8,40},{9,... | collective-permute-start | bytes 393224 | tf_op jit(solution)/shard_map/ppermute | solution.py:47
  (13 other events, 47.5 us)
